TPU v7x, 128 devices: a whole 4x4x4 slice. The times are simulated.
128 devices in a mesh: rep: 1, dp: 128 (over x, y, z, core).
Axes of the slice: x: 4, y: 4, z: 4, core: 2. Of those that a mesh axis runs over, the one named last changes fastest.
Arguments:
- g_w_gate: bfloat16 [128, 2, 512, 8192], P(('rep', 'dp'))
- g_w_up: bfloat16 [128, 2, 512, 8192], P(('rep', 'dp'))
- g_w_down: bfloat16 [128, 2, 8192, 512], P(('rep', 'dp'))
- w_gate: bfloat16 [2, 512, 8192], replicated
- w_up: bfloat16 [2, 512, 8192], replicated
- w_down: bfloat16 [2, 8192, 512], replicated
- m_w_gate: float32 [2, 512, 8192], P(None, 'dp')
- m_w_up: float32 [2, 512, 8192], P(None, 'dp')
- m_w_down: float32 [2, 8192, 512], P(None, 'dp')
- v_w_gate: float32 [2, 512, 8192], P(None, 'dp')
- v_w_up: float32 [2, 512, 8192], P(None, 'dp')
- v_w_down: float32 [2, 8192, 512], P(None, 'dp')
Outputs:
- output 1: bfloat16 [2, 512, 8192], P('rep')
- output 2: bfloat16 [2, 512, 8192], P('rep')
- output 3: bfloat16 [2, 8192, 512], P('rep')
- output 4: float32 [2, 512, 8192], P('rep', 'dp')
- output 5: float32 [2, 512, 8192], P('rep', 'dp')
- output 6: float32 [2, 8192, 512], P('rep', 'dp')
- output 7: float32 [2, 512, 8192], P('rep', 'dp')
- output 8: float32 [2, 512, 8192], P('rep', 'dp')
- output 9: float32 [2, 8192, 512], P('rep', 'dp')
All inputs are finite; a program needn't handle non-finite values.
Results may differ from a plain program's by a relative error of at most 0.022.
Values are sent between devices in bfloat16 or wider.
A program may use at most 1.5 GiB of HBM per device.

v0:
```python
import jax
import jax.numpy as jnp
from jax import lax
from jax.sharding import PartitionSpec as P


def adamw(w, m, v, g):
    m = 0.9 * m + 0.1 * g
    v = 0.95 * v + 0.05 * g * g
    step = m * lax.rsqrt(v + 1e-8) + 0.1 * w
    return (w - 0.02 * step).astype(jnp.bfloat16), m, v


def solution(mesh):
    def step(*arrays):
        terms, weights, m, v = (arrays[i : i + 3] for i in (0, 3, 6, 9))
        gradients = [lax.psum_scatter(t[0], "dp", scatter_dimension=1, tiled=True).astype(jnp.float32) for t in terms]
        me = lax.axis_index("dp")
        own = [lax.dynamic_slice_in_dim(w, me * one.shape[1], one.shape[1], 1).astype(jnp.float32) for w, one in zip(weights, m, strict=True)]
        new = [adamw(w, m, v, g) for w, m, v, g in zip(own, m, v, gradients, strict=True)]
        whole = [lax.all_gather(one[0], "dp", axis=1, tiled=True) for one in new]
        return (*whole, *(one[1] for one in new), *(one[2] for one in new))

    all_of, cut = P(None, None, None), P(None, "dp", None)
    return jax.shard_map(
        step,
        mesh=mesh,
        in_specs=(P(("rep", "dp"), None, None, None),) * 3 + (all_of,) * 3 + (cut,) * 6,
        out_specs=(P("rep", None, None),) * 3 + (P("rep", "dp", None),) * 6,
        check_vma=False,
    )
```

profile of v0, /device:TPU:1, one launch (start us, length us, event | category | flops | bytes accessed | tf_op | source)
XLA Modules:
  0.0 1237.9 jit_solution(3498944730549862536)
XLA Ops:
  7.2 0.0 all-reduce.5.cloned.1.call-start
  7.2 0.7 all-reduce.5.cloned.1.call-update
  7.9 0.0 copy-start
  7.9 0.0 copy-start.1
  7.9 0.0 copy-start.2
  7.9 0.0 copy-start.3
  8.0 0.0 copy-start.4
  8.0 0.0 copy-start.5
  8.0 0.0 reduce-scatter.4.cloned.1.call-start
  8.0 0.7 reduce-scatter.4.cloned.1.call-update
  8.7 0.0 all-gather.4.cloned.1.call-start
  8.8 293.1 %all-reduce.5.cloned.1.call-done = (bf16[2,512,8192]{2,1,0:T(8,128)(2,1)}, bf16[2,512,8192]{2,1,0:T(8,128)(2,1)}) async-done(((bf16[2,512,8192]{2,1,0:T(8,128)(2,1)}, bf16[2,512,8192]{2,1,0:T(8,128)(2,1)}), (bf16[2,512,8192]{2,1,0:T(8,128)(2,1)}, bf16[2,512,8192]{2,1,0:T(8,128)(2,1)})) %all-reduce.5.cloned.1.call-update) | async-done | bytes 33554448
  301.9 2.2 fusion.2
  304.1 0.8 copy.21
  304.8 0.0 all-gather.4.cloned.1.call-update
  304.9 0.0 all-gather.6.cloned.1.call-start
  304.9 0.0 copy-done.2
  304.9 0.0 copy-done.3
  304.9 2.2 fusion.6
  307.1 0.8 copy.22
  307.9 0.0 all-gather.6.cloned.1.call-update
  307.9 0.0 all-gather.8.cloned.1.call-start
  308.0 659.7 %reduce-scatter.4.cloned.1.call-done = bf16[2,64,512]{2,1,0:T(8,128)(2,1)} async-done(((bf16[2,8192,512]{2,1,0:T(8,128)(2,1)}), bf16[2,64,512]{2,1,0:T(8,128)(2,1)}) %reduce-scatter.4.cloned.1.call-update) | async-done | bytes 131088 | tf_op jit(solution)/shard_map/reduce_scatter | solution.py:17
  967.7 0.0 copy-done.4
  967.7 1.9 fusion.10
  969.6 0.0 all-gather.8.cloned.1.call-update
  969.6 82.5 %all-gather.4.cloned.1.call-done = bf16[2,512,8192]{2,0,1:T(2,128)(2,1)} async-done(((bf16[2,4,8192]{2,0,1:T(2,128)(2,1)}), bf16[2,512,8192]{2,0,1:T(2,128)(2,1)}) %all-gather.4.cloned.1.call-update) | async-done | bytes 16777232 | tf_op jit(solution)/shard_map/all_gather | solution.py:21
  1052.1 18.5 %copy.23 = bf16[2,512,8192]{2,1,0:T(8,128)(2,1)} copy(bf16[2,512,8192]{2,0,1:T(2,128)(2,1)} %all-gather.4.cloned.1.call-done) | data formatting | bytes 33554432
  1070.6 64.2 %all-gather.6.cloned.1.call-done = bf16[2,512,8192]{2,0,1:T(2,128)(2,1)} async-done(((bf16[2,4,8192]{2,0,1:T(2,128)(2,1)}), bf16[2,512,8192]{2,0,1:T(2,128)(2,1)}) %all-gather.6.cloned.1.call-update) | async-done | bytes 16777232 | tf_op jit(solution)/shard_map/all_gather | solution.py:21
  1134.9 18.5 %copy.24 = bf16[2,512,8192]{2,1,0:T(8,128)(2,1)} copy(bf16[2,512,8192]{2,0,1:T(2,128)(2,1)} %all-gather.6.cloned.1.call-done) | data formatting | bytes 33554432
  1153.4 64.2 %all-gather.8.cloned.1.call-done = bf16[2,8192,512]{2,1,0:T(8,128)(2,1)} async-done(((bf16[2,64,512]{2,1,0:T(8,128)(2,1)}), bf16[2,8192,512]{2,1,0:T(8,128)(2,1)}) %all-gather.8.cloned.1.call-update) | async-done | bytes 16777232 | tf_op jit(solution)/shard_map/all_gather | solution.py:21
  1217.5 13.8 %copy.34 = bf16[2,8192,512]{2,1,0:T(8,128)(2,1)} copy(bf16[2,8192,512]{2,1,0:T(8,128)(2,1)} %all-gather.8.cloned.1.call-done) | data formatting | bytes 33554432
  (3 shorter events, 0.0 us)
Async XLA Ops:
  7.2 294.7 %all-reduce.5.cloned.1.call-start = ((), (), s32[]{:S(2)}) async-start(), calls=%async_computation.5 | async-start | bytes 67108864
  7.9 294.0 %copy-start = (f32[2,4,8192]{2,1,0:T(4,128)S(1)}, f32[2,4,8192]{2,1,0:T(4,128)}, u32[]{:S(2)}) copy-start(f32[2,4,8192]{2,1,0:T(4,128)} %param.21) | copy-start | bytes 786436
  7.9 294.0 %copy-start.1 = (f32[2,4,8192]{2,1,0:T(4,128)S(1)}, f32[2,4,8192]{2,1,0:T(4,128)}, u32[]{:S(2)}) copy-start(f32[2,4,8192]{2,1,0:T(4,128)} %param.18) | copy-start | bytes 786436
  7.9 297.0 %copy-start.2 = (f32[2,4,8192]{2,1,0:T(4,128)S(1)}, f32[2,4,8192]{2,1,0:T(4,128)}, u32[]{:S(2)}) copy-start(f32[2,4,8192]{2,1,0:T(4,128)} %param.22) | copy-start | bytes 786436
  7.9 297.0 %copy-start.3 = (f32[2,4,8192]{2,1,0:T(4,128)S(1)}, f32[2,4,8192]{2,1,0:T(4,128)}, u32[]{:S(2)}) copy-start(f32[2,4,8192]{2,1,0:T(4,128)} %param.19) | copy-start | bytes 786436
  8.0 959.8 %copy-start.4 = (f32[2,64,512]{2,1,0:T(8,128)S(1)}, f32[2,64,512]{2,1,0:T(8,128)}, u32[]{:S(2)}) copy-start(f32[2,64,512]{2,1,0:T(8,128)} %param.23) | copy-start | bytes 786436
  8.0 959.7 %copy-start.5 = (f32[2,64,512]{2,1,0:T(8,128)S(1)}, f32[2,64,512]{2,1,0:T(8,128)}, u32[]{:S(2)}) copy-start(f32[2,64,512]{2,1,0:T(8,128)} %param.20) | copy-start | bytes 786436
  8.0 959.7 %reduce-scatter.4.cloned.1.call-start = ((), (), s32[]{:S(2)}) async-start(), calls=%async_computation.3 | async-start | bytes 16908288 | tf_op jit(solution)/shard_map/reduce_scatter | solution.py:17
  8.7 1043.4 %all-gather.4.cloned.1.call-start = ((), (), s32[]{:S(2)}) async-start(), calls=%async_computation.1 | async-start | bytes 16908288 | tf_op jit(solution)/shard_map/all_gather | solution.py:21
  304.9 830.0 %all-gather.6.cloned.1.call-start = ((), (), s32[]{:S(2)}) async-start(), calls=%async_computation.2 | async-start | bytes 16908288 | tf_op jit(solution)/shard_map/all_gather | solution.py:21
  307.9 909.6 %all-gather.8.cloned.1.call-start = ((), (), s32[]{:S(2)}) async-start(), calls=%async_computation.4 | async-start | bytes 16908288 | tf_op jit(solution)/shard_map/all_gather | solution.py:21
Sparse Core Ops, SparseCore 0:
  13.9 287.9 all-reduce.4
  304.3 663.4 reduce-scatter.3
  971.4 80.6 all-gather.3
  1055.7 79.1 all-gather.5
  1137.7 79.7 all-gather.7
where the time goes:
time: 1240 us
  waiting for transfers between devices  1170 us (94%)
  local copies, waits for them, and re-layouts  52.5 us (4%)
  between operations  13.9 us (1%)
    reduce_scatter x1, waiting for transfers between devices, step(): lax.psum_scatter(t[0], 'dp', scatter_dimension=1, tiled=True)  660 us
    unnamed x6, waiting for transfers between devices  295 us
    all_gather x3, waiting for transfers between devices, step(): whole = [lax.all_gather(one[0], 'dp', axis=1, tiled=True) for one in new]  211 us
    unnamed x15, local copies, waits for them, and re-layouts  50.9 us
  transfers between devices with their start and end apart: 5, of which 5 were waited for; matrix products, arithmetic and copies ran while one was open for 4% of the time, Pallas kernels for 0%

commit v1 on v0

v1 whole, which is shorter than its diff:
```python
import functools

import jax
import jax.numpy as jnp
from jax import lax
from jax.experimental import pallas as pl
from jax.experimental.pallas import tpu as pltpu
from jax.sharding import PartitionSpec as P

N = 4
MESH = pl.DeviceIdType.MESH
ORDER = ((0, 1, 2), (1, 2, 0), (2, 0, 1))
SIDES = (1, -1)
WEIGHTS = range(3)


def adamw(w, m, v, g):
    m = 0.9 * m + 0.1 * g
    v = 0.95 * v + 0.05 * g * g
    step = m * lax.rsqrt(v + 1e-8) + 0.1 * w
    return w - 0.02 * step, m, v


def place():
    me = lax.axis_index("dp")
    core = lax.rem(me, 2)
    chip = me // 2
    return (chip // (N * N), lax.rem(chip // N, N), lax.rem(chip, N)), core


def device(chip, core):
    return {"dp": ((chip[0] * N + chip[1]) * N + chip[2]) * 2 + core}


def neighbour(chip, core, axis, side):
    moved = list(chip)
    moved[axis] = lax.rem(chip[axis] + side + N, N)
    return device(moved, core)


def greet(chip, core):
    barrier = pltpu.get_barrier_semaphore()
    others = [device(chip, 1 - core)] + [neighbour(chip, core, axis, side) for axis in range(3) for side in SIDES]
    for other in others:
        pl.semaphore_signal(barrier, inc=1, device_id=other, device_id_type=MESH)
    pl.semaphore_wait(barrier, len(others))


def piece(ref, k, layer, i1, i2, h):
    if k == 2:
        return ref.at[layer, i2, :, i1, h]
    half = ref.shape[-1] // 2
    columns = pl.ds(pl.multiple_of(h * half, half), half)
    if k == 0:
        return ref.at[layer, i1, i2, :, :, columns]
    return ref.at[layer, :, i1, i2, :, columns]


def far(m):
    return (4 - m) // 2


def half_of(side, m):
    h = lax.rem(m, 2) * (1 - m // 2) if not isinstance(m, int) else (m % 2) * (1 - m // 2)
    return h if side == 1 else 1 - h


def target(mine, side, m):
    return lax.rem(mine + side * far(m) + N, N)


def turn(mine, s):
    return lax.rem(mine + 2 - s + (s // 2) * (2 * s - 1) + N, N)


def put_sum(out, sources):
    def one(out, sources):
        total = sources[0][...].astype(jnp.float32)
        for source in sources[1:]:
            total = total + source[...].astype(jnp.float32)
        out[...] = total.astype(out.dtype)

    if len(out.shape) == 2:
        one(out, sources)
    else:

        @pl.loop(0, out.shape[0])
        def _(i):
            one(out.at[i], [source.at[i] for source in sources])


def scatter_kernel(*refs):
    g, out = refs[0:3], refs[3:6]
    part, r1, r2, r3, ahead, kept = (refs[6 + 3 * i : 9 + 3 * i] for i in range(6))
    part_in, part_out, in1, out1, in2, out2, in3, out3, ahead_in, kept_in, swap_in, swap_out = refs[24:]
    chip, core = place()
    partner = device(chip, 1 - core)
    at = [[chip[axis] for axis in ORDER[k]] for k in WEIGHTS]
    lanes = [(k, d, side) for d, side in enumerate(SIDES) for k in WEIGHTS]
    greet(chip, core)

    def split(t):
        return t // N, lax.rem(t, N)

    def spot(k, side, t):
        m, s = split(t)
        return target(at[k][0], side, m), turn(at[k][1], s), half_of(side, m)

    def give(t):
        for k, d, side in lanes:
            i1, i2, h = spot(k, side, t)
            pltpu.make_async_remote_copy(
                src_ref=piece(g[k], k, 1 - core, i1, i2, h),
                dst_ref=part[k].at[i1, i2, h],
                send_sem=part_out.at[k],
                recv_sem=part_in.at[k, i1, i2, h],
                device_id=partner,
                device_id_type=MESH,
            ).start()

    def fetch(t):
        for k, d, side in lanes:
            i1, i2, h = spot(k, side, t)
            slot = lax.rem(t, 2)
            yield pltpu.make_async_copy(piece(g[k], k, core, i1, i2, h), ahead[k].at[slot, d], ahead_in.at[k, slot, d])

    def part_arrived(k, i1, i2, h):
        ref = part[k].at[i1, i2, h]
        pltpu.make_async_copy(ref, ref, part_in.at[k, i1, i2, h]).wait()

    def arrived(ref, sem):
        pltpu.make_async_copy(ref, ref, sem).wait()

    def send(k, axis, side, src, dst, out_sem, in_sem):
        pltpu.make_async_remote_copy(
            src_ref=src, dst_ref=dst, send_sem=out_sem, recv_sem=in_sem,
            device_id=neighbour(chip, core, ORDER[k][axis], side), device_id_type=MESH,
        ).start()

    @pl.loop(0, N)
    def _(t):
        give(t)

    for copy in fetch(0):
        copy.start()

    def own_copies():
        for k in WEIGHTS:
            for i2 in range(N):
                for h in range(2):
                    yield pltpu.make_async_copy(piece(g[k], k, core, at[k][0], i2, h), kept[k].at[i2, h], kept_in.at[k])

    def first(last):
        def body(t):
            give(t + N)
            if last:

                @pl.when(t + 1 < 3 * N)
                def _():
                    for copy in fetch(t + 1):
                        copy.start()
            else:
                for copy in fetch(t + 1):
                    copy.start()
            pending = None
            for (k, d, side), copy in zip(lanes, fetch(t), strict=True):
                i1, i2, h = spot(k, side, t)
                copy.wait()
                part_arrived(k, i1, i2, h)
                here = part[k].at[i1, i2, h]
                sources = [here, ahead[k].at[lax.rem(t, 2), d]]
                if last:
                    arrived(r1[k].at[d, 0, i2], in1.at[k, d, 0, i2])
                    sources.append(r1[k].at[d, 0, i2])
                put_sum(here, sources)
                if pending is not None:
                    pending()
                m = 2 if last else t // N
                pending = functools.partial(send, k, 0, side, here, r1[k].at[d, m, i2], out1.at[k, d], in1.at[k, d, m, i2])
            pending()

        return body

    pl.loop(0, 2 * N)(first(False))
    for copy in own_copies():
        copy.start()
    pl.loop(2 * N, 3 * N)(first(True))

    for k in WEIGHTS:
        pltpu.make_async_copy(kept[k], kept[k], kept_in.at[k]).wait()

    def settled(k, side, m):
        i2, h = target(at[k][1], side, m), half_of(side, m)
        part_arrived(k, at[k][0], i2, h)
        for d, m1 in ((0, 2 - h), (1, 1 + h)):
            arrived(r1[k].at[d, m1, i2], in1.at[k, d, m1, i2])

    def terms1(k, i2, h, i3):
        here = part[k].at[at[k][0], i2, h, i3]
        return here, [here, kept[k].at[i2, h, i3], r1[k].at[0, 2 - h, i2, i3], r1[k].at[1, 1 + h, i2, i3]]

    for m in range(3):
        for k, d, side in lanes:
            settled(k, side, m)

        @pl.loop(0, N)
        def _(s):
            pending = None
            for k, d, side in lanes:
                i2, h, i3 = target(at[k][1], side, m), half_of(side, m), turn(at[k][2], s)
                here, sources = terms1(k, i2, h, i3)
                if m == 2:
                    arrived(r2[k].at[d, 0, i3], in2.at[k, d, 0, i3])
                    sources.append(r2[k].at[d, 0, i3])
                put_sum(here, sources)
                if pending is not None:
                    pending()
                pending = functools.partial(send, k, 1, side, here, r2[k].at[d, m, i3], out2.at[k, d], in2.at[k, d, m, i3])
            pending()

    for k, d, side in lanes:
        settled(k, side, 3)
    for m in range(4):
        pending = None
        for k, d, side in lanes:
            i2, h, i3 = at[k][1], half_of(side, m), target(at[k][2], side, m)
            here, sources = terms1(k, i2, h, i3)
            for e, m2 in ((0, 2 - h), (1, 1 + h)):
                arrived(r2[k].at[e, m2, i3], in2.at[k, e, m2, i3])
                sources.append(r2[k].at[e, m2, i3])
            if m == 2:
                arrived(r3[k].at[d, 0], in3.at[k, d, 0])
                sources.append(r3[k].at[d, 0])
            if m == 3:
                for e, m3 in ((0, 2 - h), (1, 1 + h)):
                    arrived(r3[k].at[e, m3], in3.at[k, e, m3])
                    sources.append(r3[k].at[e, m3])
                here = out[k].at[core, h]
            put_sum(here, sources)
            if pending is not None:
                pending()
            pending = None
            if m < 3:
                pending = functools.partial(send, k, 2, side, here, r3[k].at[d, m], out3.at[k, d], in3.at[k, d, m])
        if pending is not None:
            pending()

    swaps = [
        pltpu.make_async_remote_copy(
            src_ref=out[k].at[core], dst_ref=out[k].at[core], send_sem=swap_out.at[k], recv_sem=swap_in.at[k],
            device_id=partner, device_id_type=MESH,
        )
        for k in WEIGHTS
    ]
    for swap in swaps:
        swap.start()
    for k in WEIGHTS:
        pltpu.make_async_copy(part[k], part[k], part_out.at[k]).wait()
        for d in range(2):
            arrived(r1[k].at[d], out1.at[k, d])
            arrived(r2[k].at[d], out2.at[k, d])
            arrived(r3[k].at[d], out3.at[k, d])
    for k, swap in zip(WEIGHTS, swaps, strict=True):
        swap.wait_send()
        arrived(out[k].at[1 - core], swap_in.at[k])


def gather_kernel(*refs):
    new, own, other = refs[0:3], refs[3:6], refs[6:9]
    theirs = refs[9:11]
    in1, out1, in2, out2, in3, out3, pass_in, pass_out, swap_in, swap_out = refs[11:]
    chip, core = place()
    partner = device(chip, 1 - core)
    at = [[chip[axis] for axis in ORDER[k]] for k in WEIGHTS]
    lanes = [(k, d, side) for d, side in enumerate(SIDES) for k in WEIGHTS]
    greet(chip, core)

    def arrived(ref, sem):
        pltpu.make_async_copy(ref, ref, sem).wait()

    p, q, r = zip(*at, strict=True)
    landing = [theirs[0], theirs[1], own[2].at[p[2], q[2], core, r[2]]]
    for k in WEIGHTS:
        pltpu.make_async_remote_copy(
            src_ref=new[k].at[1 - core], dst_ref=landing[k], send_sem=swap_out.at[k], recv_sem=swap_in.at[k],
            device_id=partner, device_id_type=MESH,
        ).start()
    own[2][p[2], q[2], core, r[2]] = new[2][core]
    for k in range(2):
        arrived(theirs[k], swap_in.at[k])
        half = own[k].shape[-1]
        for h in range(2):
            columns = pl.ds(h * half, half)
            mine, yours = new[k][core, :, columns], theirs[k][:, columns]
            low, high = jnp.where(core == 0, mine, yours), jnp.where(core == 0, yours, mine)
            own[k][p[k], q[k], h, r[k]] = jnp.concatenate([low, high], axis=0).astype(jnp.bfloat16)
    arrived(own[2].at[p[2], q[2], 1 - core, r[2]], swap_in.at[2])

    def send(k, axis, side, ref, out_sem, in_sem):
        pltpu.make_async_remote_copy(
            src_ref=ref, dst_ref=ref, send_sem=out_sem, recv_sem=in_sem,
            device_id=neighbour(chip, core, ORDER[k][axis], side), device_id_type=MESH,
        ).start()

    def source(mine, side, m):
        return mine if m < 2 else lax.rem(mine - side + N, N)

    def send3(k, d, side, m):
        i3, h = source(r[k], side, m), half_of(side, m)
        send(k, 2, side, own[k].at[p[k], q[k], h, i3], out3.at[k, d], in3.at[k, d, m])

    def send2(k, d, side, m, i3):
        i2, h = source(q[k], side, m), half_of(side, m)
        send(k, 1, side, own[k].at[p[k], i2, h, i3], out2.at[k, d], in2.at[k, d, m, i3])

    def send1(k, d, side, m, i2):
        i1, h = source(p[k], side, m), half_of(side, m)
        send(k, 0, side, own[k].at[i1, i2, h], out1.at[k, d], in1.at[k, d, m, i2])

    def await3(k, d, m):
        arrived(r_block(k), in3.at[k, d, m])

    def await2(k, d, m, i3):
        arrived(r_block(k), in2.at[k, d, m, i3])

    def await1(k, d, m, i2):
        arrived(own[k].at[0, 0, 0], in1.at[k, d, m, i2])

    def r_block(k):
        return own[k].at[0, 0, 0, 0]

    def hand(k, i1, i2):
        pltpu.make_async_remote_copy(
            src_ref=own[k].at[i1, i2], dst_ref=other[k].at[i1, i2], send_sem=pass_out.at[k], recv_sem=pass_in.at[k],
            device_id=partner, device_id_type=MESH,
        ).start()

    def step(mine, offset):
        return lax.rem(mine + offset + N, N)

    for m in range(2):
        for k, d, side in lanes:
            send3(k, d, side, m)
    for m in range(2):
        for k, d, side in lanes:
            send2(k, d, side, m, r[k])
    for k, d, side in lanes:
        await3(k, d, 0)
        send3(k, d, side, 2)
    for behind in SIDES:
        e = SIDES.index(behind)
        for k in WEIGHTS:
            await3(k, e, 1)
        for m in range(2):
            for k, d, side in lanes:
                send2(k, d, side, m, step(r[k], -behind))
    for k, d, side in lanes:
        await3(k, d, 2)
    for m in range(2):
        for k, d, side in lanes:
            send2(k, d, side, m, step(r[k], 2))
    for m in range(2):
        for k, d, side in lanes:
            send1(k, d, side, m, q[k])
    for k in WEIGHTS:
        hand(k, p[k], q[k])
    for offset in (0, -1, 1, 2):
        for k, d, side in lanes:
            await2(k, d, 0, step(r[k], offset))
            send2(k, d, side, 2, step(r[k], offset))
    for behind in SIDES:
        e = SIDES.index(behind)
        for offset in (0, -1, 1, 2):
            for k in WEIGHTS:
                await2(k, e, 1, step(r[k], offset))
        for m in range(2):
            for k, d, side in lanes:
                send1(k, d, side, m, step(q[k], -behind))
        for k in WEIGHTS:
            hand(k, p[k], step(q[k], -behind))
    for offset in (0, -1, 1, 2):
        for k, d, side in lanes:
            await2(k, d, 2, step(r[k], offset))
    for m in range(2):
        for k, d, side in lanes:
            send1(k, d, side, m, step(q[k], 2))
    for k in WEIGHTS:
        hand(k, p[k], step(q[k], 2))
    for offset in (0, -1, 1, 2):
        for k, d, side in lanes:
            await1(k, d, 0, step(q[k], offset))
            send1(k, d, side, 2, step(q[k], offset))
    for offset in (0, -1, 1, 2):
        for k, d, side in lanes:
            await1(k, d, 1, step(q[k], offset))
            hand(k, step(p[k], -side), step(q[k], offset))
    for offset in (0, -1, 1, 2):
        for k in WEIGHTS:
            for d in range(2):
                await1(k, d, 2, step(q[k], offset))
            hand(k, step(p[k], 2), step(q[k], offset))

    for k in WEIGHTS:
        arrived(new[k].at[0], swap_out.at[k])
        for d in range(2):
            arrived(own[k].at[0:3, :, 0], out1.at[k, d])
            arrived(own[k].at[0, 0:3, 0], out2.at[k, d])
            arrived(own[k].at[0, 0, 0, 0:3], out3.at[k, d])
        arrived(own[k], pass_out.at[k])
        arrived(other[k], pass_in.at[k])


def write_kernel(*refs):
    own, other, out, sem = refs[0:3], refs[3:6], refs[6:9], refs[9]
    _, core = place()
    copies = []
    for i1 in range(N):
        for i2 in range(N):
            for h in range(2):
                for k in WEIGHTS:
                    copies.append(pltpu.make_async_copy(own[k].at[i1, i2, h], piece(out[k], k, core, i1, i2, h), sem.at[k, 0]))
                    copies.append(pltpu.make_async_copy(other[k].at[i1, i2, h], piece(out[k], k, 1 - core, i1, i2, h), sem.at[k, 1]))
    for copy in copies:
        copy.start()
    for k in WEIGHTS:
        pltpu.make_async_copy(own[k], own[k], sem.at[k, 0]).wait()
        pltpu.make_async_copy(other[k], other[k], sem.at[k, 1]).wait()


ANY = pl.BlockSpec(memory_space=pl.ANY)
VMEM = pl.BlockSpec(memory_space=pltpu.VMEM)
LIMIT = 67_000_000
SMALL = 4 * 2**20


def scatter(terms):
    bf16, dma = jnp.bfloat16, pltpu.SemaphoreType.DMA
    blocks = [(t.shape[-2], t.shape[-1] // 2) if k < 2 else t.shape[-2:] for k, t in enumerate(terms)]
    each = lambda *lead: [pltpu.VMEM((*lead, *b), bf16) for b in blocks]
    return pl.pallas_call(
        scatter_kernel,
        out_shape=[jax.ShapeDtypeStruct((2, 2, *b), bf16) for b in blocks],
        in_specs=[ANY] * 3,
        out_specs=[VMEM] * 3,
        scratch_shapes=[
            *each(N, N, 2, N), *each(2, 3, N, N), *each(2, 3, N), *each(2, 3), *each(2, 2, N), *each(N, 2, N),
            dma((3, N, N, 2)), dma((3,)),
            dma((3, 2, 3, N)), dma((3, 2)),
            dma((3, 2, 3, N)), dma((3, 2)),
            dma((3, 2, 3)), dma((3, 2)),
            dma((3, 2, 2)), dma((3,)), dma((3,)), dma((3,)),
        ],
        compiler_params=pltpu.CompilerParams(collective_id=0, has_side_effects=True, vmem_limit_bytes=LIMIT),
        name="scatter",
    )(*terms)


def gather(new):
    bf16, dma = jnp.bfloat16, pltpu.SemaphoreType.DMA
    blocks = [(2 * n.shape[1], n.shape[2] // 2) if k < 2 else n.shape[1:] for k, n in enumerate(new)]
    whole = [pltpu.VMEM((N, N, 2, N, *b), bf16) for b in blocks]
    return pl.pallas_call(
        gather_kernel,
        out_shape=whole * 2,
        in_specs=[VMEM] * 3,
        out_specs=[VMEM] * 6,
        scratch_shapes=[
            *(pltpu.VMEM(n.shape[1:], n.dtype) for n in new[:2]),
            dma((3, 2, 3, N)), dma((3, 2)),
            dma((3, 2, 3, N)), dma((3, 2)),
            dma((3, 2, 3)), dma((3, 2)),
            dma((3,)), dma((3,)), dma((3,)), dma((3,)),
        ],
        compiler_params=pltpu.CompilerParams(collective_id=1, has_side_effects=True, vmem_limit_bytes=SMALL),
        name="gather",
    )(*new)


def write(gathered, shapes):
    return pl.pallas_call(
        write_kernel,
        out_shape=[jax.ShapeDtypeStruct(s, jnp.bfloat16) for s in shapes],
        in_specs=[VMEM] * 6,
        out_specs=[ANY] * 3,
        scratch_shapes=[pltpu.SemaphoreType.DMA((3, 2))],
        compiler_params=pltpu.CompilerParams(vmem_limit_bytes=SMALL),
        name="write",
    )(*gathered)


def solution(mesh):
    def step(*arrays):
        terms, weights, m, v = (arrays[i : i + 3] for i in (0, 3, 6, 9))
        core = lax.rem(lax.axis_index("dp"), 2)
        me = lax.axis_index("dp")
        views = []
        for k, t in enumerate(terms):
            _, layers, rows, columns = t.shape
            block = rows // N**3
            views.append((layers, N, N, N, block, columns) if k < 2 else (layers, N, N, N, 2, block // 2, columns))
        sums = scatter([t.reshape(view) for t, view in zip(terms, views, strict=True)])
        gradients = []
        for k, total in enumerate(sums):
            if k < 2:
                layers, _, rows, half = total.shape
                total = total.transpose(0, 2, 1, 3).reshape(layers, 2, rows // 2, 2 * half)
            gradients.append(lax.dynamic_index_in_dim(total, core, 1, keepdims=False).astype(jnp.float32))
        own = [lax.dynamic_slice_in_dim(w, me * one.shape[1], one.shape[1], 1).astype(jnp.float32) for w, one in zip(weights, m, strict=True)]
        new = [adamw(*one) for one in zip(own, m, v, gradients, strict=True)]
        rows = [one[0].astype(jnp.bfloat16).astype(jnp.float32) if k < 2 else one[0].astype(jnp.bfloat16) for k, one in enumerate(new)]
        whole = write(gather(rows), views)
        whole = [w.reshape(t.shape[1:]) for w, t in zip(whole, terms, strict=True)]
        return (*whole, *(one[1] for one in new), *(one[2] for one in new))

    all_of, cut = P(None, None, None), P(None, "dp", None)
    return jax.shard_map(
        step,
        mesh=mesh,
        in_specs=(P(("rep", "dp"), None, None, None),) * 3 + (all_of,) * 3 + (cut,) * 6,
        out_specs=(P("rep", None, None),) * 3 + (P("rep", "dp", None),) * 6,
        check_vma=False,
    )
```

time: 1240 us -> 232 us (0.19)
  waiting for transfers between devices: 1170 us -> 0 us
  Pallas kernels: 0 us -> 224 us
  local copies, waits for them, and re-layouts: 52.5 us -> 2.78 us
  between operations: 13.9 us -> 0.69 us
    reduce_scatter x1 -> x0, waiting for transfers between devices: 660 us -> none  [step(): lax.psum_scatter(t[0], 'dp', scatter_dimension=1, tiled=True)]
    unnamed x6 -> x0, waiting for transfers between devices: 295 us -> none
    pallas_call x0 -> x3, Pallas kernels: none -> 224 us  [the longest x1 108 us: scatter(): pl.pallas_call(scatter_kernel, out_shape=[jax.ShapeDtypeStruct((2, 2, *b)...]
    all_gather x3 -> x0, waiting for transfers between devices: 211 us -> none  [step(): whole = [lax.all_gather(one[0], 'dp', axis=1, tiled=True) for one in new]]
    unnamed x15 -> x0, local copies, waits for them, and re-layouts: 50.9 us -> none
  transfers between devices with their start and end apart: 5 -> 0, of which waited for: 5 -> 0; matrix products, arithmetic and copies ran while one was open for 4% -> 0% of each run, Pallas kernels for 0% -> 0%
where the time goes in v1:
time: 232 us
  Pallas kernels  224 us (97%)
  other arithmetic  4.96 us (2%)
  local copies, waits for them, and re-layouts  2.78 us (1%)
    pallas_call x1, Pallas kernels, scatter(): pl.pallas_call(scatter_kernel, out_shape=[jax.ShapeDtypeStruct((2, 2, *b)...  108 us
    pallas_call x1, Pallas kernels, gather(): pl.pallas_call(gather_kernel, out_shape=whole * 2, in_specs=[VMEM] * 3, o...  99.5 us
    pallas_call x1, Pallas kernels, write(): pl.pallas_call(write_kernel, out_shape=[jax.ShapeDtypeStruct(s, jnp.bfloa...  15.9 us

profile of v1, /device:TPU:1, one launch (start us, length us, event | category | flops | bytes accessed | tf_op | source)
XLA Modules:
  0.0 232.2 jit_solution(3125864587249826185)
XLA Ops:
  0.7 108.4 %scatter.1 = (bf16[2,2,8,4096]{3,2,1,0:T(8,128)(2,1)}, bf16[2,2,8,4096]{3,2,1,0:T(8,128)(2,1)}, bf16[2,2,64,512]{3,2,1,0:T(8,128)(2,1)}) custom-call(bf16[2,4,4,4,8,8192]{5,4,3,2,1,0:T(8,128)(2,1)} %bitcast.30, bf16[2,4,4,4,8,8192]{5,4,3,2,1,0:T(8,128)(2,1)} %bitcast.31, bf16[2,4,4,4,2,64,512]{6,5,4,3,2,1,0:T(8,128)(2,1)} %bitcast.32), custom_call_target="tpu_custom_call" | custom-call | tf_op jit(solution)/shard_map/scatter/pallas_call | solution.py:440
  109.1 1.2 copy.22
  110.3 0.2 reshape.51
  110.5 1.2 copy.24
  111.7 0.2 reshape.52
  111.9 2.1 fusion.8
  114.0 2.9 %fusion.15 = (f32[2,4,8192]{2,1,0:T(4,128)S(1)}, f32[2,4,8192]{2,1,0:T(4,128)}, f32[2,4,8192]{2,1,0:T(4,128)}, f32[2,4,8192]{2,1,0:T(4,128)S(1)}, f32[2,4,8192]{2,1,0:T(4,128)}, /*index=5*/f32[2,4,8192]{2,1,0:T(4,128)}) fusion(bf16[2,512,8192]{2,1,0:T(8,128)(2,1)} %param.16, s32[]{:T(128)S(6)} %select_n.14, bf16[2,2,4,8192]{3,2,1,0:T(4,128)(2,1)S(1)} %reshape.52, ...), kind=kLoop, calls=%fused_computation.30 | loop fusion | flops 2228224 | bytes 3145736 | tf_op jit(solution)/shard_map/convert_element_type | solution.py:510
  116.9 99.5 %gather.1 = (bf16[4,4,2,4,8,4096]{5,4,3,2,1,0:T(8,128)(2,1)S(1)}, bf16[4,4,2,4,8,4096]{5,4,3,2,1,0:T(8,128)(2,1)S(1)}, bf16[4,4,2,4,64,512]{5,4,3,2,1,0:T(8,128)...) custom-call(f32[2,4,8192]{2,1,0:T(4,128)S(1)} %get-tuple-element.42., ...), custom_call_target="tpu_custom_call" | custom-call | tf_op jit(solution)/shard_map/gather/pallas_call | solution.py:462
  216.4 15.9 %write.1 = (bf16[2,4,4,4,8,8192]{5,4,3,2,1,0:T(8,128)(2,1)}, bf16[2,4,4,4,8,8192]{5,4,3,2,1,0:T(8,128)(2,1)}, bf16[2,4,4,4,2,64,512]{6,5,4,3,2,1,0:T(8,128)(2,1)}) custom-call(bf16[4,4,2,4,8,4096]{5,4,3,2,1,0:T(8,128)(2,1)S(1)} %get-tuple-element.24.refs_0_, bf16[4,4,2,4,8,4096]{5,4,3,2,1,0:T(8,128)(2,1)S(1)} %get-tuple-element.25.refs_1_, ...), custom_call_target="tpu_custom_call" | custom-call | tf_op jit(solution)/shard_map/write/pallas_call | solution.py:480

commit v2 on v1

v2 whole, which is shorter than its diff:
```python
import functools

import jax
import jax.numpy as jnp
from jax import lax
from jax.experimental import pallas as pl
from jax.experimental.pallas import tpu as pltpu
from jax.sharding import PartitionSpec as P

N = 4
MESH = pl.DeviceIdType.MESH
ORDER = ((0, 1, 2), (1, 2, 0), (2, 0, 1))
SIDES = (1, -1)
WEIGHTS = range(3)


def adamw(w, m, v, g):
    m = 0.9 * m + 0.1 * g
    v = 0.95 * v + 0.05 * g * g
    step = m * lax.rsqrt(v + 1e-8) + 0.1 * w
    return w - 0.02 * step, m, v


def place():
    me = lax.axis_index("dp")
    core = lax.rem(me, 2)
    chip = me // 2
    return (chip // (N * N), lax.rem(chip // N, N), lax.rem(chip, N)), core


def device(chip, core):
    return {"dp": ((chip[0] * N + chip[1]) * N + chip[2]) * 2 + core}


def neighbour(chip, core, axis, side):
    moved = list(chip)
    moved[axis] = lax.rem(chip[axis] + side + N, N)
    return device(moved, core)


def greet(chip, core):
    barrier = pltpu.get_barrier_semaphore()
    others = [device(chip, 1 - core)] + [neighbour(chip, core, axis, side) for axis in range(3) for side in SIDES]
    for other in others:
        pl.semaphore_signal(barrier, inc=1, device_id=other, device_id_type=MESH)
    pl.semaphore_wait(barrier, len(others))


def piece(ref, k, layer, i1, i2, h):
    if k == 2:
        return ref.at[layer, i2, :, i1, h]
    half = ref.shape[-1] // 2
    columns = pl.ds(pl.multiple_of(h * half, half), half)
    if k == 0:
        return ref.at[layer, i1, i2, :, :, columns]
    return ref.at[layer, :, i1, i2, :, columns]


def far(m):
    return (4 - m) // 2


def half_of(side, m):
    h = lax.rem(m, 2) * (1 - m // 2) if not isinstance(m, int) else (m % 2) * (1 - m // 2)
    return h if side == 1 else 1 - h


def target(mine, side, m):
    return lax.rem(mine + side * far(m) + N, N)


def turn(mine, s):
    return lax.rem(mine + 2 - s + (s // 2) * (2 * s - 1) + N, N)


def put_sum(out, sources):
    def one(out, sources):
        total = sources[0][...].astype(jnp.float32)
        for source in sources[1:]:
            total = total + source[...].astype(jnp.float32)
        out[...] = total.astype(out.dtype)

    if len(out.shape) == 2:
        one(out, sources)
    else:

        @pl.loop(0, out.shape[0])
        def _(i):
            one(out.at[i], [source.at[i] for source in sources])


def rows_of_both(core, mine, theirs):
    low, high = jnp.where(core == 0, mine, theirs), jnp.where(core == 0, theirs, mine)
    return jnp.concatenate([low, high], axis=0)


def step_kernel(*refs):
    g, w, moments = refs[0:3], refs[3:6], (refs[6:9], refs[9:12])
    own, other, fresh = refs[12:15], refs[15:18], (refs[18:21], refs[21:24])
    ahead, kept, grad, weight = (refs[24 + 3 * i : 27 + 3 * i] for i in range(4))
    mine, theirs = ((refs[36 + 6 * i : 39 + 6 * i], refs[39 + 6 * i : 42 + 6 * i]) for i in range(2))
    part_in, part_out, rs1_in, rs1_out, rs2_in, rs2_out, rs3_in, rs3_out, ahead_in, kept_in = refs[48:58]
    weight_in, mine_in, theirs_in, theirs_out, grad_in, grad_out = refs[58:64]
    in1, out1, in2, out2, in3, out3, pass_in, pass_out, ready = refs[64:73]
    chip, core = place()
    partner = device(chip, 1 - core)
    at = [[chip[axis] for axis in ORDER[k]] for k in WEIGHTS]
    p, q, r = zip(*at, strict=True)
    lanes = [(k, d, side) for d, side in enumerate(SIDES) for k in WEIGHTS]

    def flat(i1, i2, h):
        return (i1 * N + i2) * 2 + h

    def arrived(ref, sem):
        pltpu.make_async_copy(ref, ref, sem).wait()

    def push(src, dst, out_sem, in_sem, where):
        pltpu.make_async_remote_copy(
            src_ref=src, dst_ref=dst, send_sem=out_sem, recv_sem=in_sem, device_id=where, device_id_type=MESH
        ).start()

    def send(k, axis, side, src, dst, out_sem, in_sem):
        push(src, dst, out_sem, in_sem, neighbour(chip, core, ORDER[k][axis], side))

    def r1(k, d, m, i2):
        return other[k].at[(d * 3 + m) * N + i2]

    def r2(k, d, m, i3):
        return other[k].at[24 + d * 3 + m, i3]

    def r3(k, d, m):
        return other[k].at[30 + d, m]

    def spot(k, side, t):
        m, s = t // N, lax.rem(t, N)
        return target(p[k], side, m), turn(q[k], s), half_of(side, m)

    def give(t):
        for k, d, side in lanes:
            i1, i2, h = spot(k, side, t)
            push(piece(g[k], k, 1 - core, i1, i2, h), own[k].at[flat(i1, i2, h)], part_out.at[k], part_in.at[k, flat(i1, i2, h)], partner)

    def fetch(t):
        for k, d, side in lanes:
            i1, i2, h = spot(k, side, t)
            slot = lax.rem(t, 2)
            yield pltpu.make_async_copy(piece(g[k], k, core, i1, i2, h), ahead[k].at[slot, d], ahead_in.at[k, slot, d])

    def part_arrived(k, i1, i2, h):
        arrived(own[k].at[flat(i1, i2, h)], part_in.at[k, flat(i1, i2, h)])

    small = [pltpu.make_async_copy(w[k].at[core, chip[0], chip[1], chip[2]], weight[k], weight_in.at[k]) for k in WEIGHTS]
    small += [pltpu.make_async_copy(moments[i][k], mine[i][k], mine_in.at[i, k]) for i in range(2) for k in WEIGHTS]
    for copy in fetch(0):
        copy.start()
    greet(chip, core)

    @pl.loop(0, N)
    def _(t):
        give(t)

    for copy in small:
        copy.start()
    for i in range(2):
        for k in WEIGHTS:
            push(moments[i][k].at[1 - core], theirs[i][k], theirs_out.at[i, k], theirs_in.at[i, k], partner)

    def first(last):
        def body(t):
            give(t + N)
            if last:

                @pl.when(t + 1 < 3 * N)
                def _():
                    for copy in fetch(t + 1):
                        copy.start()
            else:
                for copy in fetch(t + 1):
                    copy.start()
            pending = None
            for (k, d, side), copy in zip(lanes, fetch(t), strict=True):
                i1, i2, h = spot(k, side, t)
                copy.wait()
                part_arrived(k, i1, i2, h)
                here = own[k].at[flat(i1, i2, h)]
                sources = [here, ahead[k].at[lax.rem(t, 2), d]]
                if last:
                    arrived(r1(k, d, 0, i2), rs1_in.at[k, d, 0, i2])
                    sources.append(r1(k, d, 0, i2))
                put_sum(here, sources)
                if pending is not None:
                    pending()
                m = 2 if last else t // N
                pending = functools.partial(send, k, 0, side, here, r1(k, d, m, i2), rs1_out.at[k, d], rs1_in.at[k, d, m, i2])
            pending()

        return body

    pl.loop(0, 2 * N)(first(False))
    for k in WEIGHTS:
        for i2 in range(N):
            for h in range(2):
                pltpu.make_async_copy(piece(g[k], k, core, p[k], i2, h), kept[k].at[i2, h], kept_in.at[k]).start()
    pl.loop(2 * N, 3 * N)(first(True))

    for k in WEIGHTS:
        arrived(kept[k], kept_in.at[k])

    def settled(k, side, m):
        i2, h = target(q[k], side, m), half_of(side, m)
        part_arrived(k, p[k], i2, h)
        for d, m1 in ((0, 2 - h), (1, 1 + h)):
            arrived(r1(k, d, m1, i2), rs1_in.at[k, d, m1, i2])

    def terms(k, i2, h, i3):
        here = own[k].at[flat(p[k], i2, h), i3]
        return here, [here, kept[k].at[i2, h, i3], r1(k, 0, 2 - h, i2).at[i3], r1(k, 1, 1 + h, i2).at[i3]]

    for m in range(3):
        for k, d, side in lanes:
            settled(k, side, m)

        @pl.loop(0, N)
        def _(s):
            pending = None
            for k, d, side in lanes:
                i2, h, i3 = target(q[k], side, m), half_of(side, m), turn(r[k], s)
                here, sources = terms(k, i2, h, i3)
                if m == 2:
                    arrived(r2(k, d, 0, i3), rs2_in.at[k, d, 0, i3])
                    sources.append(r2(k, d, 0, i3))
                put_sum(here, sources)
                if pending is not None:
                    pending()
                pending = functools.partial(send, k, 1, side, here, r2(k, d, m, i3), rs2_out.at[k, d], rs2_in.at[k, d, m, i3])
            pending()

    for copy in small:
        copy.wait()
    for i in range(2):
        for k in WEIGHTS:
            arrived(theirs[i][k], theirs_in.at[i, k])
    for k, d, side in lanes:
        settled(k, side, 3)
    for m in range(4):
        pending = None
        for k, d, side in lanes:
            h, i3 = half_of(side, m), target(r[k], side, m)
            here, sources = terms(k, q[k], h, i3)
            for e, m2 in ((0, 2 - h), (1, 1 + h)):
                arrived(r2(k, e, m2, i3), rs2_in.at[k, e, m2, i3])
                sources.append(r2(k, e, m2, i3))
            if m == 2:
                arrived(r3(k, d, 0), rs3_in.at[k, d, 0])
                sources.append(r3(k, d, 0))
            if m == 3:
                for e, m3 in ((0, 2 - h), (1, 1 + h)):
                    arrived(r3(k, e, m3), rs3_in.at[k, e, m3])
                    sources.append(r3(k, e, m3))
                here = grad[k].at[core, h]
            put_sum(here, sources)
            if pending is not None:
                pending()
            pending = None
            if m < 3:
                pending = functools.partial(send, k, 2, side, here, r3(k, d, m), rs3_out.at[k, d], rs3_in.at[k, d, m])
        if pending is not None:
            pending()

    for k in WEIGHTS:
        for d in range(2):
            arrived(own[k].at[0:12], rs1_out.at[k, d])
            arrived(own[k].at[0:3], rs2_out.at[k, d])
            arrived(own[k].at[0, 0:3], rs3_out.at[k, d])
    for where in [partner] + [neighbour(chip, core, axis, side) for axis in range(3) for side in SIDES]:
        pl.semaphore_signal(ready, inc=1, device_id=where, device_id_type=MESH)

    for k in range(2):
        half = own[k].shape[-1]
        width = min(half, 1024)
        for h in range(2):
            block = own[k].at[flat(p[k], q[k], h), r[k]]

            @pl.loop(0, half // width)
            def _(c):
                within = pl.ds(pl.multiple_of(c * width, width), width)
                columns = pl.ds(pl.multiple_of(h * half + c * width, width), width)
                m, v = (rows_of_both(core, mine[i][k][core, :, columns], theirs[i][k][:, columns]) for i in range(2))
                new, _, _ = adamw(weight[k][:, columns].astype(jnp.float32), m, v, grad[k][core, h, :, within].astype(jnp.float32))
                block[:, within] = new.astype(block.dtype)

    depth = min(own[2].shape[-2], 16)
    for h in range(2):
        block = own[2].at[flat(p[2], q[2], h), r[2]]

        @pl.loop(0, own[2].shape[-2] // depth)
        def _(c):
            rows = pl.ds(pl.multiple_of(c * depth, depth), depth)
            m, v = (jnp.where(core == h, mine[i][2][core, rows], theirs[i][2][rows]) for i in range(2))
            new, _, _ = adamw(weight[2][h, rows].astype(jnp.float32), m, v, grad[2][core, h, rows].astype(jnp.float32))
            block[rows] = new.astype(block.dtype)

    for k in WEIGHTS:
        push(grad[k].at[core], grad[k].at[core], grad_out.at[k], grad_in.at[k], partner)
    pl.semaphore_wait(ready, 7)

    def source(mine, side, m):
        return mine if m < 2 else lax.rem(mine - side + N, N)

    def send3(k, d, side, m):
        i3, h = source(r[k], side, m), half_of(side, m)
        ref = own[k].at[flat(p[k], q[k], h), i3]
        send(k, 2, side, ref, ref, out3.at[k, d], in3.at[k, d, m])

    def send2(k, d, side, m, i3):
        i2, h = source(q[k], side, m), half_of(side, m)
        ref = own[k].at[flat(p[k], i2, h), i3]
        send(k, 1, side, ref, ref, out2.at[k, d], in2.at[k, d, m, i3])

    def send1(k, d, side, m, i2):
        i1, h = source(p[k], side, m), half_of(side, m)
        ref = own[k].at[flat(i1, i2, h)]
        send(k, 0, side, ref, ref, out1.at[k, d], in1.at[k, d, m, i2])

    def await3(k, d, m):
        arrived(own[k].at[0, 0], in3.at[k, d, m])

    def await2(k, d, m, i3):
        arrived(own[k].at[0, 0], in2.at[k, d, m, i3])

    def await1(k, d, m, i2):
        arrived(own[k].at[0], in1.at[k, d, m, i2])

    def hand(k, i1, i2):
        both = pl.ds(flat(i1, i2, 0), 2)
        push(own[k].at[both], other[k].at[both], pass_out.at[k], pass_in.at[k], partner)

    def step(mine, offset):
        return lax.rem(mine + offset + N, N)

    for m in range(2):
        for k, d, side in lanes:
            send3(k, d, side, m)
    for m in range(2):
        for k, d, side in lanes:
            send2(k, d, side, m, r[k])
    for k, d, side in lanes:
        await3(k, d, 0)
        send3(k, d, side, 2)
    for e, behind in enumerate(SIDES):
        for k in WEIGHTS:
            await3(k, e, 1)
        for m in range(2):
            for k, d, side in lanes:
                send2(k, d, side, m, step(r[k], -behind))
    for k, d, side in lanes:
        await3(k, d, 2)
    for m in range(2):
        for k, d, side in lanes:
            send2(k, d, side, m, step(r[k], 2))
    for m in range(2):
        for k, d, side in lanes:
            send1(k, d, side, m, q[k])
    for k in WEIGHTS:
        hand(k, p[k], q[k])

    for k in WEIGHTS:
        arrived(grad[k].at[1 - core], grad_in.at[k])
    for layer in range(2):
        for k in range(2):
            half = own[k].shape[-1]
            width = min(half, 1024)
            for h in range(2):

                @pl.loop(0, half // width)
                def _(c):
                    within = pl.ds(pl.multiple_of(c * width, width), width)
                    columns = pl.ds(pl.multiple_of(h * half + c * width, width), width)
                    total = grad[k][layer, h, :, within].astype(jnp.float32)
                    rows = total.shape[0] // 2
                    total = jnp.where(core == 0, total[:rows], total[rows:])
                    _, m, v = adamw(total, mine[0][k][layer, :, columns], mine[1][k][layer, :, columns], total)
                    fresh[0][k][layer, :, columns] = m
                    fresh[1][k][layer, :, columns] = v

        @pl.loop(0, own[2].shape[-2] // depth)
        def _(c):
            rows = pl.ds(pl.multiple_of(c * depth, depth), depth)
            total = grad[2][layer, core, rows].astype(jnp.float32)
            _, m, v = adamw(total, mine[0][2][layer, rows], mine[1][2][layer, rows], total)
            fresh[0][2][layer, rows] = m
            fresh[1][2][layer, rows] = v

    for offset in (0, -1, 1, 2):
        for k, d, side in lanes:
            await2(k, d, 0, step(r[k], offset))
            send2(k, d, side, 2, step(r[k], offset))
    for e, behind in enumerate(SIDES):
        for offset in (0, -1, 1, 2):
            for k in WEIGHTS:
                await2(k, e, 1, step(r[k], offset))
        for m in range(2):
            for k, d, side in lanes:
                send1(k, d, side, m, step(q[k], -behind))
        for k in WEIGHTS:
            hand(k, p[k], step(q[k], -behind))
    for offset in (0, -1, 1, 2):
        for k, d, side in lanes:
            await2(k, d, 2, step(r[k], offset))
    for m in range(2):
        for k, d, side in lanes:
            send1(k, d, side, m, step(q[k], 2))
    for k in WEIGHTS:
        hand(k, p[k], step(q[k], 2))
    for offset in (0, -1, 1, 2):
        for k, d, side in lanes:
            await1(k, d, 0, step(q[k], offset))
            send1(k, d, side, 2, step(q[k], offset))
    for offset in (0, -1, 1, 2):
        for k, d, side in lanes:
            await1(k, d, 1, step(q[k], offset))
            hand(k, step(p[k], -side), step(q[k], offset))
    for offset in (0, -1, 1, 2):
        for k in WEIGHTS:
            for d in range(2):
                await1(k, d, 2, step(q[k], offset))
            hand(k, step(p[k], 2), step(q[k], offset))

    for k in WEIGHTS:
        arrived(own[k], part_out.at[k])
        arrived(grad[k].at[0], grad_out.at[k])
        for i in range(2):
            arrived(theirs[i][k], theirs_out.at[i, k])
        for d in range(2):
            arrived(own[k].at[0:12], out1.at[k, d])
            arrived(own[k].at[0:3], out2.at[k, d])
            arrived(own[k].at[0, 0:3], out3.at[k, d])
        arrived(own[k], pass_out.at[k])
        arrived(other[k], pass_in.at[k])


def write_kernel(*refs):
    own, other, moments, out, written, sem, moment_sem = refs[0:3], refs[3:6], refs[6:12], refs[12:15], refs[15:21], refs[21], refs[22]
    _, core = place()
    copies = []
    for i1 in range(N):
        for i2 in range(N):
            for h in range(2):
                for k in WEIGHTS:
                    j = (i1 * N + i2) * 2 + h
                    copies.append(pltpu.make_async_copy(own[k].at[j], piece(out[k], k, core, i1, i2, h), sem.at[k, 0]))
                    copies.append(pltpu.make_async_copy(other[k].at[j], piece(out[k], k, 1 - core, i1, i2, h), sem.at[k, 1]))
    small = [pltpu.make_async_copy(a, b, moment_sem.at[i]) for i, (a, b) in enumerate(zip(moments, written, strict=True))]
    for copy in copies + small:
        copy.start()
    for k in WEIGHTS:
        pltpu.make_async_copy(own[k], own[k], sem.at[k, 0]).wait()
        pltpu.make_async_copy(other[k], other[k], sem.at[k, 1]).wait()
    for copy in small:
        copy.wait()


ANY = pl.BlockSpec(memory_space=pl.ANY)
VMEM = pl.BlockSpec(memory_space=pltpu.VMEM)
LIMIT = 14 * 2**20
SMALL = 2**20


def solution(mesh):
    bf16, f32, dma = jnp.bfloat16, jnp.float32, pltpu.SemaphoreType.DMA

    def step(*arrays):
        terms, weights, m, v = (arrays[i : i + 3] for i in (0, 3, 6, 9))
        views, blocks = [], []
        for k, w in enumerate(weights):
            layers, rows, columns = w.shape
            block = rows // N**3
            views.append((layers, N, N, N, block, columns) if k < 2 else (layers, N, N, N, 2, block // 2, columns))
            blocks.append((block, columns // 2) if k < 2 else (block // 2, columns))
        each = lambda *lead: [pltpu.VMEM((*lead, *b), bf16) for b in blocks]
        moment = [pltpu.VMEM(one.shape, f32) for one in (*m, *v)]
        layer = [pltpu.VMEM(one.shape[1:], f32) for one in (*m, *v)]
        results = pl.pallas_call(
            step_kernel,
            out_shape=[*each(2 * N * N, N), *each(2 * N * N, N), *moment],
            in_specs=[ANY] * 12,
            out_specs=[VMEM] * 12,
            scratch_shapes=[
                *each(2, 2, N), *each(N, 2, N), *each(2, 2), *(pltpu.VMEM(view[4:], bf16) for view in views),
                *moment, *layer,
                dma((3, 2 * N * N)), dma((3,)),
                dma((3, 2, 3, N)), dma((3, 2)),
                dma((3, 2, 3, N)), dma((3, 2)),
                dma((3, 2, 3)), dma((3, 2)),
                dma((3, 2, 2)), dma((3,)),
                dma((3,)), dma((2, 3)), dma((2, 3)), dma((2, 3)), dma((3,)), dma((3,)),
                dma((3, 2, 3, N)), dma((3, 2)),
                dma((3, 2, 3, N)), dma((3, 2)),
                dma((3, 2, 3)), dma((3, 2)),
                dma((3,)), dma((3,)), pltpu.SemaphoreType.REGULAR,
            ],
            compiler_params=pltpu.CompilerParams(collective_id=0, has_side_effects=True, vmem_limit_bytes=LIMIT),
            name="step",
        )(*(t.reshape(view) for t, view in zip(terms, views, strict=True)), *(w.reshape(view) for w, view in zip(weights, views, strict=True)), *m, *v)
        out = pl.pallas_call(
            write_kernel,
            out_shape=[*(jax.ShapeDtypeStruct(view, bf16) for view in views), *(jax.ShapeDtypeStruct(one.shape, f32) for one in (*m, *v))],
            in_specs=[VMEM] * 12,
            out_specs=[ANY] * 9,
            scratch_shapes=[dma((3, 2)), dma((6,))],
            compiler_params=pltpu.CompilerParams(vmem_limit_bytes=SMALL),
            name="write",
        )(*results)
        return (*(w.reshape(old.shape) for w, old in zip(out[:3], weights, strict=True)), *out[3:])

    all_of, cut = P(None, None, None), P(None, "dp", None)
    return jax.shard_map(
        step,
        mesh=mesh,
        in_specs=(P(("rep", "dp"), None, None, None),) * 3 + (all_of,) * 3 + (cut,) * 6,
        out_specs=(P("rep", None, None),) * 3 + (P("rep", "dp", None),) * 6,
        check_vma=False,
    )
```

time: 232 us -> 255 us (1.099)
  local copies, waits for them, and re-layouts: 2.78 us -> 33.5 us
  other arithmetic: 4.96 us -> 0 us
  Pallas kernels: 224 us -> 221 us
    unnamed x0 -> x20, local copies, waits for them, and re-layouts: none -> 33.5 us
    convert_element_type x2 -> x0, other arithmetic: 4.96 us -> none  [the longest x1 2.89 us: step(): one[0].astype(jnp.bfloat16).astype(jnp.float32)]
    pallas_call x3 -> x2, Pallas kernels: 224 us -> 221 us  [the longest x1 204 us: step(): pl.pallas_call(step_kernel, out_shape=[*each(2 * N * N, N), *each(2 * N *...]
where the time goes in v2:
time: 255 us
  Pallas kernels  221 us (87%)
  local copies, waits for them, and re-layouts  33.5 us (13%)
    pallas_call x1, Pallas kernels, step(): pl.pallas_call(step_kernel, out_shape=[*each(2 * N * N, N), *each(2 * N *...  204 us
    unnamed x20, local copies, waits for them, and re-layouts  33.5 us
    pallas_call x1, Pallas kernels, step(): pl.pallas_call(write_kernel, out_shape=[*(jax.ShapeDtypeStruct(view, bf16...  16.4 us

profile of v2, /device:TPU:1, one launch (start us, length us, event | category | flops | bytes accessed | tf_op | source)
XLA Modules:
  0.0 254.7 jit_solution(2387845811598971094)
XLA Ops:
  0.6 204.1 %step.1 = (bf16[32,4,8,4096]{3,2,1,0:T(8,128)(2,1)S(1)}, bf16[32,4,8,4096]{3,2,1,0:T(8,128)(2,1)S(1)}, bf16[32,4,64,512]{3,2,1,0:T(8,128)(2,1)S(1)}, bf16[32,4,8...) custom-call(bf16[2,4,4,4,8,8192]{5,4,3,2,1,0:T(8,128)(2,1)} %bitcast, ...), custom_call_target="tpu_custom_call" | custom-call | tf_op jit(solution)/shard_map/step/pallas_call | solution.py:483
  204.8 0.0 copy-start
  204.8 3.4 %copy-done = bf16[32,4,8,4096]{3,2,1,0:T(8,128)(2,1)} copy-done((bf16[32,4,8,4096]{3,2,1,0:T(8,128)(2,1)}, bf16[32,4,8,4096]{3,2,1,0:T(8,128)(2,1)S(1)}, u32[]{:S(2)}) %copy-start) | copy-done | bytes 8388632
  208.2 0.0 copy-start.2
  208.2 3.4 %copy-done.2 = bf16[32,4,8,4096]{3,2,1,0:T(8,128)(2,1)} copy-done((bf16[32,4,8,4096]{3,2,1,0:T(8,128)(2,1)}, bf16[32,4,8,4096]{3,2,1,0:T(8,128)(2,1)S(1)}, u32[]{:S(2)}) %copy-start.2) | copy-done | bytes 8388632
  211.6 0.0 copy-start.4
  211.6 3.4 %copy-done.4 = bf16[32,4,64,512]{3,2,1,0:T(8,128)(2,1)} copy-done((bf16[32,4,64,512]{3,2,1,0:T(8,128)(2,1)}, bf16[32,4,64,512]{3,2,1,0:T(8,128)(2,1)S(1)}, u32[]{:S(2)}) %copy-start.4) | copy-done | bytes 8388632
  215.0 0.0 copy-start.6
  215.0 3.2 %copy-done.6 = bf16[32,4,8,4096]{3,2,1,0:T(8,128)(2,1)} copy-done((bf16[32,4,8,4096]{3,2,1,0:T(8,128)(2,1)}, bf16[32,4,8,4096]{3,2,1,0:T(8,128)(2,1)S(1)}, u32[]{:S(2)}) %copy-start.6) | copy-done | bytes 8388632
  218.2 0.0 copy-start.8
  218.2 3.2 %copy-done.8 = bf16[32,4,8,4096]{3,2,1,0:T(8,128)(2,1)} copy-done((bf16[32,4,8,4096]{3,2,1,0:T(8,128)(2,1)}, bf16[32,4,8,4096]{3,2,1,0:T(8,128)(2,1)S(1)}, u32[]{:S(2)}) %copy-start.8) | copy-done | bytes 8388632
  221.4 0.0 copy-start.1
  221.4 3.4 %copy-done.1 = bf16[32,4,8,4096]{3,2,1,0:T(8,128)(2,1)S(1)} copy-done((bf16[32,4,8,4096]{3,2,1,0:T(8,128)(2,1)S(1)}, bf16[32,4,8,4096]{3,2,1,0:T(8,128)(2,1)}, u32[]{:S(2)}) %copy-start.1) | copy-done | bytes 8388632
  224.8 0.0 copy-start.3
  224.8 3.4 %copy-done.3 = bf16[32,4,8,4096]{3,2,1,0:T(8,128)(2,1)S(1)} copy-done((bf16[32,4,8,4096]{3,2,1,0:T(8,128)(2,1)S(1)}, bf16[32,4,8,4096]{3,2,1,0:T(8,128)(2,1)}, u32[]{:S(2)}) %copy-start.3) | copy-done | bytes 8388632
  228.2 0.0 copy-start.5
  228.2 3.4 %copy-done.5 = bf16[32,4,64,512]{3,2,1,0:T(8,128)(2,1)S(1)} copy-done((bf16[32,4,64,512]{3,2,1,0:T(8,128)(2,1)S(1)}, bf16[32,4,64,512]{3,2,1,0:T(8,128)(2,1)}, u32[]{:S(2)}) %copy-start.5) | copy-done | bytes 8388632
  231.6 0.0 copy-start.7
  231.6 3.4 %copy-done.7 = bf16[32,4,8,4096]{3,2,1,0:T(8,128)(2,1)S(1)} copy-done((bf16[32,4,8,4096]{3,2,1,0:T(8,128)(2,1)S(1)}, bf16[32,4,8,4096]{3,2,1,0:T(8,128)(2,1)}, u32[]{:S(2)}) %copy-start.7) | copy-done | bytes 8388632
  235.0 0.0 copy-start.9
  235.0 3.4 %copy-done.9 = bf16[32,4,8,4096]{3,2,1,0:T(8,128)(2,1)S(1)} copy-done((bf16[32,4,8,4096]{3,2,1,0:T(8,128)(2,1)S(1)}, bf16[32,4,8,4096]{3,2,1,0:T(8,128)(2,1)}, u32[]{:S(2)}) %copy-start.9) | copy-done | bytes 8388632
  238.3 16.4 %write.1 = (bf16[2,4,4,4,8,8192]{5,4,3,2,1,0:T(8,128)(2,1)}, bf16[2,4,4,4,8,8192]{5,4,3,2,1,0:T(8,128)(2,1)}, bf16[2,4,4,4,2,64,512]{6,5,4,3,2,1,0:T(8,128)(2,1)...) custom-call(bf16[32,4,8,4096]{3,2,1,0:T(8,128)(2,1)S(1)} %copy-done., ...), custom_call_target="tpu_custom_call" | custom-call | tf_op jit(solution)/shard_map/write/pallas_call | solution.py:505
Async XLA Ops:
  204.8 3.4 %copy-start = (bf16[32,4,8,4096]{3,2,1,0:T(8,128)(2,1)}, bf16[32,4,8,4096]{3,2,1,0:T(8,128)(2,1)S(1)}, u32[]{:S(2)}) copy-start(bf16[32,4,8,4096]{3,2,1,0:T(8,128)(2,1)S(1)} %get-tuple-element.30.refs_0_) | copy-start | bytes 25165828
  208.2 3.4 %copy-start.2 = (bf16[32,4,8,4096]{3,2,1,0:T(8,128)(2,1)}, bf16[32,4,8,4096]{3,2,1,0:T(8,128)(2,1)S(1)}, u32[]{:S(2)}) copy-start(bf16[32,4,8,4096]{3,2,1,0:T(8,128)(2,1)S(1)} %get-tuple-element.31.refs_1_) | copy-start | bytes 25165828
  211.6 3.4 %copy-start.4 = (bf16[32,4,64,512]{3,2,1,0:T(8,128)(2,1)}, bf16[32,4,64,512]{3,2,1,0:T(8,128)(2,1)S(1)}, u32[]{:S(2)}) copy-start(bf16[32,4,64,512]{3,2,1,0:T(8,128)(2,1)S(1)} %get-tuple-element.32.refs_2_) | copy-start | bytes 25165828
  215.0 3.2 %copy-start.6 = (bf16[32,4,8,4096]{3,2,1,0:T(8,128)(2,1)}, bf16[32,4,8,4096]{3,2,1,0:T(8,128)(2,1)S(1)}, u32[]{:S(2)}) copy-start(bf16[32,4,8,4096]{3,2,1,0:T(8,128)(2,1)S(1)} %get-tuple-element.33.refs_3_) | copy-start | bytes 25165828
  218.2 3.2 %copy-start.8 = (bf16[32,4,8,4096]{3,2,1,0:T(8,128)(2,1)}, bf16[32,4,8,4096]{3,2,1,0:T(8,128)(2,1)S(1)}, u32[]{:S(2)}) copy-start(bf16[32,4,8,4096]{3,2,1,0:T(8,128)(2,1)S(1)} %get-tuple-element.34.refs_4_) | copy-start | bytes 25165828
  221.4 3.4 %copy-start.1 = (bf16[32,4,8,4096]{3,2,1,0:T(8,128)(2,1)S(1)}, bf16[32,4,8,4096]{3,2,1,0:T(8,128)(2,1)}, u32[]{:S(2)}) copy-start(bf16[32,4,8,4096]{3,2,1,0:T(8,128)(2,1)} %copy-done) | copy-start | bytes 25165828
  224.8 3.4 %copy-start.3 = (bf16[32,4,8,4096]{3,2,1,0:T(8,128)(2,1)S(1)}, bf16[32,4,8,4096]{3,2,1,0:T(8,128)(2,1)}, u32[]{:S(2)}) copy-start(bf16[32,4,8,4096]{3,2,1,0:T(8,128)(2,1)} %copy-done.2) | copy-start | bytes 25165828
  228.2 3.4 %copy-start.5 = (bf16[32,4,64,512]{3,2,1,0:T(8,128)(2,1)S(1)}, bf16[32,4,64,512]{3,2,1,0:T(8,128)(2,1)}, u32[]{:S(2)}) copy-start(bf16[32,4,64,512]{3,2,1,0:T(8,128)(2,1)} %copy-done.4) | copy-start | bytes 25165828
  231.6 3.4 %copy-start.7 = (bf16[32,4,8,4096]{3,2,1,0:T(8,128)(2,1)S(1)}, bf16[32,4,8,4096]{3,2,1,0:T(8,128)(2,1)}, u32[]{:S(2)}) copy-start(bf16[32,4,8,4096]{3,2,1,0:T(8,128)(2,1)} %copy-done.6) | copy-start | bytes 25165828
  235.0 3.4 %copy-start.9 = (bf16[32,4,8,4096]{3,2,1,0:T(8,128)(2,1)S(1)}, bf16[32,4,8,4096]{3,2,1,0:T(8,128)(2,1)}, u32[]{:S(2)}) copy-start(bf16[32,4,8,4096]{3,2,1,0:T(8,128)(2,1)} %copy-done.8) | copy-start | bytes 25165828

commit v3 on v2

--- a/solution.py
+++ b/solution.py
@@ -97,11 +97,11 @@
 def step_kernel(*refs):
     g, w, moments = refs[0:3], refs[3:6], (refs[6:9], refs[9:12])
     own, other, fresh = refs[12:15], refs[15:18], (refs[18:21], refs[21:24])
-    ahead, kept, grad, weight = (refs[24 + 3 * i : 27 + 3 * i] for i in range(4))
-    mine, theirs = ((refs[36 + 6 * i : 39 + 6 * i], refs[39 + 6 * i : 42 + 6 * i]) for i in range(2))
-    part_in, part_out, rs1_in, rs1_out, rs2_in, rs2_out, rs3_in, rs3_out, ahead_in, kept_in = refs[48:58]
-    weight_in, mine_in, theirs_in, theirs_out, grad_in, grad_out = refs[58:64]
-    in1, out1, in2, out2, in3, out3, pass_in, pass_out, ready = refs[64:73]
+    ahead, grad, weight = (refs[24 + 3 * i : 27 + 3 * i] for i in range(3))
+    theirs = (refs[33:36], refs[36:39])
+    part_in, part_out, rs1_in, rs1_out, rs2_in, rs2_out, rs3_in, rs3_out, ahead_in = refs[39:48]
+    weight_in, fresh_in, theirs_in, theirs_out, grad_in, grad_out = refs[48:54]
+    in1, out1, in2, out2, in3, out3, pass_in, pass_out, ready = refs[54:63]
     chip, core = place()
     partner = device(chip, 1 - core)
     at = [[chip[axis] for axis in ORDER[k]] for k in WEIGHTS]
@@ -150,7 +150,7 @@
         arrived(own[k].at[flat(i1, i2, h)], part_in.at[k, flat(i1, i2, h)])
 
     small = [pltpu.make_async_copy(w[k].at[core, chip[0], chip[1], chip[2]], weight[k], weight_in.at[k]) for k in WEIGHTS]
-    small += [pltpu.make_async_copy(moments[i][k], mine[i][k], mine_in.at[i, k]) for i in range(2) for k in WEIGHTS]
+    small += [pltpu.make_async_copy(moments[i][k], fresh[i][k], fresh_in.at[i, k]) for i in range(2) for k in WEIGHTS]
     for copy in fetch(0):
         copy.start()
     greet(chip, core)
@@ -197,14 +197,15 @@
         return body
 
     pl.loop(0, 2 * N)(first(False))
-    for k in WEIGHTS:
-        for i2 in range(N):
-            for h in range(2):
-                pltpu.make_async_copy(piece(g[k], k, core, p[k], i2, h), kept[k].at[i2, h], kept_in.at[k]).start()
     pl.loop(2 * N, 3 * N)(first(True))
 
-    for k in WEIGHTS:
-        arrived(kept[k], kept_in.at[k])
+    def fetch_kept(m):
+        for k, d, side in lanes:
+            i2, h = target(q[k], side, m), half_of(side, m)
+            yield pltpu.make_async_copy(piece(g[k], k, core, p[k], i2, h), ahead[k].at[m % 2, d], ahead_in.at[k, m % 2, d])
+
+    for copy in fetch_kept(0):
+        copy.start()
 
     def settled(k, side, m):
         i2, h = target(q[k], side, m), half_of(side, m)
@@ -212,20 +213,23 @@
         for d, m1 in ((0, 2 - h), (1, 1 + h)):
             arrived(r1(k, d, m1, i2), rs1_in.at[k, d, m1, i2])
 
-    def terms(k, i2, h, i3):
+    def terms(k, i2, h, i3, kept):
         here = own[k].at[flat(p[k], i2, h), i3]
-        return here, [here, kept[k].at[i2, h, i3], r1(k, 0, 2 - h, i2).at[i3], r1(k, 1, 1 + h, i2).at[i3]]
+        return here, [here, kept.at[i3], r1(k, 0, 2 - h, i2).at[i3], r1(k, 1, 1 + h, i2).at[i3]]
 
     for m in range(3):
-        for k, d, side in lanes:
+        for (k, d, side), copy in zip(lanes, fetch_kept(m), strict=True):
             settled(k, side, m)
+            copy.wait()
+        for copy in fetch_kept(m + 1):
+            copy.start()
 
         @pl.loop(0, N)
         def _(s):
             pending = None
             for k, d, side in lanes:
                 i2, h, i3 = target(q[k], side, m), half_of(side, m), turn(r[k], s)
-                here, sources = terms(k, i2, h, i3)
+                here, sources = terms(k, i2, h, i3, ahead[k].at[m % 2, d])
                 if m == 2:
                     arrived(r2(k, d, 0, i3), rs2_in.at[k, d, 0, i3])
                     sources.append(r2(k, d, 0, i3))
@@ -240,13 +244,14 @@
     for i in range(2):
         for k in WEIGHTS:
             arrived(theirs[i][k], theirs_in.at[i, k])
-    for k, d, side in lanes:
+    for (k, d, side), copy in zip(lanes, fetch_kept(3), strict=True):
         settled(k, side, 3)
+        copy.wait()
     for m in range(4):
         pending = None
         for k, d, side in lanes:
             h, i3 = half_of(side, m), target(r[k], side, m)
-            here, sources = terms(k, q[k], h, i3)
+            here, sources = terms(k, q[k], h, i3, ahead[k].at[1, h])
             for e, m2 in ((0, 2 - h), (1, 1 + h)):
                 arrived(r2(k, e, m2, i3), rs2_in.at[k, e, m2, i3])
                 sources.append(r2(k, e, m2, i3))
@@ -285,7 +290,7 @@
             def _(c):
                 within = pl.ds(pl.multiple_of(c * width, width), width)
                 columns = pl.ds(pl.multiple_of(h * half + c * width, width), width)
-                m, v = (rows_of_both(core, mine[i][k][core, :, columns], theirs[i][k][:, columns]) for i in range(2))
+                m, v = (rows_of_both(core, fresh[i][k][core, :, columns], theirs[i][k][:, columns]) for i in range(2))
                 new, _, _ = adamw(weight[k][:, columns].astype(jnp.float32), m, v, grad[k][core, h, :, within].astype(jnp.float32))
                 block[:, within] = new.astype(block.dtype)
 
@@ -296,7 +301,7 @@
         @pl.loop(0, own[2].shape[-2] // depth)
         def _(c):
             rows = pl.ds(pl.multiple_of(c * depth, depth), depth)
-            m, v = (jnp.where(core == h, mine[i][2][core, rows], theirs[i][2][rows]) for i in range(2))
+            m, v = (jnp.where(core == h, fresh[i][2][core, rows], theirs[i][2][rows]) for i in range(2))
             new, _, _ = adamw(weight[2][h, rows].astype(jnp.float32), m, v, grad[2][core, h, rows].astype(jnp.float32))
             block[rows] = new.astype(block.dtype)
 
@@ -379,7 +384,7 @@
                     total = grad[k][layer, h, :, within].astype(jnp.float32)
                     rows = total.shape[0] // 2
                     total = jnp.where(core == 0, total[:rows], total[rows:])
-                    _, m, v = adamw(total, mine[0][k][layer, :, columns], mine[1][k][layer, :, columns], total)
+                    _, m, v = adamw(total, fresh[0][k][layer, :, columns], fresh[1][k][layer, :, columns], total)
                     fresh[0][k][layer, :, columns] = m
                     fresh[1][k][layer, :, columns] = v
 
@@ -387,7 +392,7 @@
         def _(c):
             rows = pl.ds(pl.multiple_of(c * depth, depth), depth)
             total = grad[2][layer, core, rows].astype(jnp.float32)
-            _, m, v = adamw(total, mine[0][2][layer, rows], mine[1][2][layer, rows], total)
+            _, m, v = adamw(total, fresh[0][2][layer, rows], fresh[1][2][layer, rows], total)
             fresh[0][2][layer, rows] = m
             fresh[1][2][layer, rows] = v
 
@@ -462,7 +467,7 @@
 
 ANY = pl.BlockSpec(memory_space=pl.ANY)
 VMEM = pl.BlockSpec(memory_space=pltpu.VMEM)
-LIMIT = 14 * 2**20
+LIMIT = 6 * 2**20
 SMALL = 2**20
 
 
@@ -486,13 +491,13 @@
             in_specs=[ANY] * 12,
             out_specs=[VMEM] * 12,
             scratch_shapes=[
-                *each(2, 2, N), *each(N, 2, N), *each(2, 2), *(pltpu.VMEM(view[4:], bf16) for view in views),
-                *moment, *layer,
+                *each(2, 2, N), *each(2, 2), *(pltpu.VMEM(view[4:], bf16) for view in views),
+                *layer,
                 dma((3, 2 * N * N)), dma((3,)),
                 dma((3, 2, 3, N)), dma((3, 2)),
                 dma((3, 2, 3, N)), dma((3, 2)),
                 dma((3, 2, 3)), dma((3, 2)),
-                dma((3, 2, 2)), dma((3,)),
+                dma((3, 2, 2)),
                 dma((3,)), dma((2, 3)), dma((2, 3)), dma((2, 3)), dma((3,)), dma((3,)),
                 dma((3, 2, 3, N)), dma((3, 2)),
                 dma((3, 2, 3, N)), dma((3, 2)),

time: 255 us -> 221 us (0.87)
  local copies, waits for them, and re-layouts: 33.5 us -> 0 us
    unnamed x20 -> x0, local copies, waits for them, and re-layouts: 33.5 us -> none
where the time goes in v3:
time: 221 us
  Pallas kernels  220 us (100%)
    pallas_call x1, Pallas kernels, step(): pl.pallas_call(step_kernel, out_shape=[*each(2 * N * N, N), *each(2 * N *...  204 us
    pallas_call x1, Pallas kernels, step(): pl.pallas_call(write_kernel, out_shape=[*(jax.ShapeDtypeStruct(view, bf16...  16.4 us

profile of v3, /device:TPU:1, one launch (start us, length us, event | category | flops | bytes accessed | tf_op | source)
XLA Modules:
  0.0 221.2 jit_solution(11999738819061436553)
XLA Ops:
  0.6 204.1 %step.1 = (bf16[32,4,8,4096]{3,2,1,0:T(8,128)(2,1)S(1)}, bf16[32,4,8,4096]{3,2,1,0:T(8,128)(2,1)S(1)}, bf16[32,4,64,512]{3,2,1,0:T(8,128)(2,1)S(1)}, bf16[32,4,8...) custom-call(bf16[2,4,4,4,8,8192]{5,4,3,2,1,0:T(8,128)(2,1)} %bitcast, ...), custom_call_target="tpu_custom_call" | custom-call | tf_op jit(solution)/shard_map/step/pallas_call | solution.py:488
  204.8 16.4 %write.1 = (bf16[2,4,4,4,8,8192]{5,4,3,2,1,0:T(8,128)(2,1)}, bf16[2,4,4,4,8,8192]{5,4,3,2,1,0:T(8,128)(2,1)}, bf16[2,4,4,4,2,64,512]{6,5,4,3,2,1,0:T(8,128)(2,1)...) custom-call(bf16[32,4,8,4096]{3,2,1,0:T(8,128)(2,1)S(1)} %get-tuple-, ...), custom_call_target="tpu_custom_call" | custom-call | tf_op jit(solution)/shard_map/write/pallas_call | solution.py:510

commit v4 on v3

--- a/solution.py
+++ b/solution.py
@@ -101,7 +101,7 @@
     theirs = (refs[33:36], refs[36:39])
     part_in, part_out, rs1_in, rs1_out, rs2_in, rs2_out, rs3_in, rs3_out, ahead_in = refs[39:48]
     weight_in, fresh_in, theirs_in, theirs_out, grad_in, grad_out = refs[48:54]
-    in1, out1, in2, out2, in3, out3, pass_in, pass_out, ready = refs[54:63]
+    pass_in, pass_out, ready, first_in = refs[54:58]
     chip, core = place()
     partner = device(chip, 1 - core)
     at = [[chip[axis] for axis in ORDER[k]] for k in WEIGHTS]
@@ -135,10 +135,10 @@
         m, s = t // N, lax.rem(t, N)
         return target(p[k], side, m), turn(q[k], s), half_of(side, m)
 
-    def give(t):
+    def give(t, j):
         for k, d, side in lanes:
             i1, i2, h = spot(k, side, t)
-            push(piece(g[k], k, 1 - core, i1, i2, h), own[k].at[flat(i1, i2, h)], part_out.at[k], part_in.at[k, flat(i1, i2, h)], partner)
+            push(piece(g[k], k, 1 - core, i1, i2, h), own[k].at[flat(i1, i2, h)], part_out.at[k], part_in.at[k, d, j], partner)
 
     def fetch(t):
         for k, d, side in lanes:
@@ -146,8 +146,9 @@
             slot = lax.rem(t, 2)
             yield pltpu.make_async_copy(piece(g[k], k, core, i1, i2, h), ahead[k].at[slot, d], ahead_in.at[k, slot, d])
 
-    def part_arrived(k, i1, i2, h):
-        arrived(own[k].at[flat(i1, i2, h)], part_in.at[k, flat(i1, i2, h)])
+    def all_arrived(sem, j, pieces):
+        for k, d, side in lanes:
+            arrived(own[k].at[0:4] if pieces else own[k].at[0], sem.at[k, d, j])
 
     small = [pltpu.make_async_copy(w[k].at[core, chip[0], chip[1], chip[2]], weight[k], weight_in.at[k]) for k in WEIGHTS]
     small += [pltpu.make_async_copy(moments[i][k], fresh[i][k], fresh_in.at[i, k]) for i in range(2) for k in WEIGHTS]
@@ -155,9 +156,15 @@
         copy.start()
     greet(chip, core)
 
-    @pl.loop(0, N)
+    for i3 in range(N):
+        for k, d, side in lanes:
+            i1, i2, h = spot(k, side, 0)
+            source = piece(g[k], k, 1 - core, i1, i2, h).at[i3]
+            push(source, own[k].at[flat(i1, i2, h), i3], part_out.at[k], first_in.at[k, d, i3], partner)
+
+    @pl.loop(1, N)
     def _(t):
-        give(t)
+        give(t, t - 1)
 
     for copy in small:
         copy.start()
@@ -165,39 +172,56 @@
         for k in WEIGHTS:
             push(moments[i][k].at[1 - core], theirs[i][k], theirs_out.at[i, k], theirs_in.at[i, k], partner)
 
-    def first(last):
+    def first(m):
         def body(t):
-            give(t + N)
-            if last:
-
-                @pl.when(t + 1 < 3 * N)
-                def _():
-                    for copy in fetch(t + 1):
-                        copy.start()
-            else:
+            give(t + N, m + 3)
+
+            @pl.when(t + 1 < 3 * N)
+            def _():
                 for copy in fetch(t + 1):
                     copy.start()
+
             pending = None
             for (k, d, side), copy in zip(lanes, fetch(t), strict=True):
                 i1, i2, h = spot(k, side, t)
                 copy.wait()
-                part_arrived(k, i1, i2, h)
                 here = own[k].at[flat(i1, i2, h)]
+                if m == 0:
+                    arrived(here, part_in.at[k, d, t - 1])
                 sources = [here, ahead[k].at[lax.rem(t, 2), d]]
-                if last:
-                    arrived(r1(k, d, 0, i2), rs1_in.at[k, d, 0, i2])
+                if m == 2:
                     sources.append(r1(k, d, 0, i2))
                 put_sum(here, sources)
                 if pending is not None:
                     pending()
-                m = 2 if last else t // N
-                pending = functools.partial(send, k, 0, side, here, r1(k, d, m, i2), rs1_out.at[k, d], rs1_in.at[k, d, m, i2])
+                pending = functools.partial(send, k, 0, side, here, r1(k, d, m, i2), rs1_out.at[k, d], rs1_in.at[k, d, 2 + i2 if m == 2 else m])
             pending()
 
         return body
 
-    pl.loop(0, 2 * N)(first(False))
-    pl.loop(2 * N, 3 * N)(first(True))
+    give(N, 3)
+    for copy in fetch(1):
+        copy.start()
+    pending = None
+    copies = fetch(0)
+    for i3 in range(N):
+        for k, d, side in lanes:
+            i1, i2, h = spot(k, side, 0)
+            if i3 == 0:
+                next(copies).wait()
+            here = own[k].at[flat(i1, i2, h), i3]
+            arrived(here, first_in.at[k, d, i3])
+            put_sum(here, [here, ahead[k].at[0, d, i3]])
+            if pending is not None:
+                pending()
+            pending = functools.partial(send, k, 0, side, here, r1(k, d, 0, i2).at[i3], rs1_out.at[k, d], rs1_in.at[k, d, 0])
+    pending()
+    pl.loop(1, N)(first(0))
+    all_arrived(part_in, 3, True)
+    pl.loop(N, 2 * N)(first(1))
+    all_arrived(part_in, 4, True)
+    all_arrived(rs1_in, 0, True)
+    pl.loop(2 * N, 3 * N)(first(2))
 
     def fetch_kept(m):
         for k, d, side in lanes:
@@ -209,15 +233,17 @@
 
     def settled(k, side, m):
         i2, h = target(q[k], side, m), half_of(side, m)
-        part_arrived(k, p[k], i2, h)
-        for d, m1 in ((0, 2 - h), (1, 1 + h)):
-            arrived(r1(k, d, m1, i2), rs1_in.at[k, d, m1, i2])
+        arrived(r1(k, h, 2, i2), rs1_in.at[k, h, 2 + i2])
 
     def terms(k, i2, h, i3, kept):
         here = own[k].at[flat(p[k], i2, h), i3]
         return here, [here, kept.at[i3], r1(k, 0, 2 - h, i2).at[i3], r1(k, 1, 1 + h, i2).at[i3]]
 
+    all_arrived(part_in, 5, True)
+    all_arrived(rs1_in, 1, True)
     for m in range(3):
+        if m == 2:
+            all_arrived(rs2_in, 0, False)
         for (k, d, side), copy in zip(lanes, fetch_kept(m), strict=True):
             settled(k, side, m)
             copy.wait()
@@ -231,12 +257,11 @@
                 i2, h, i3 = target(q[k], side, m), half_of(side, m), turn(r[k], s)
                 here, sources = terms(k, i2, h, i3, ahead[k].at[m % 2, d])
                 if m == 2:
-                    arrived(r2(k, d, 0, i3), rs2_in.at[k, d, 0, i3])
                     sources.append(r2(k, d, 0, i3))
                 put_sum(here, sources)
                 if pending is not None:
                     pending()
-                pending = functools.partial(send, k, 1, side, here, r2(k, d, m, i3), rs2_out.at[k, d], rs2_in.at[k, d, m, i3])
+                pending = functools.partial(send, k, 1, side, here, r2(k, d, m, i3), rs2_out.at[k, d], rs2_in.at[k, d, 2 + i3 if m == 2 else m])
             pending()
 
     for copy in small:
@@ -247,13 +272,15 @@
     for (k, d, side), copy in zip(lanes, fetch_kept(3), strict=True):
         settled(k, side, 3)
         copy.wait()
+    all_arrived(rs2_in, 1, False)
     for m in range(4):
         pending = None
         for k, d, side in lanes:
             h, i3 = half_of(side, m), target(r[k], side, m)
             here, sources = terms(k, q[k], h, i3, ahead[k].at[1, h])
             for e, m2 in ((0, 2 - h), (1, 1 + h)):
-                arrived(r2(k, e, m2, i3), rs2_in.at[k, e, m2, i3])
+                if m2 == 2:
+                    arrived(r2(k, e, 2, i3), rs2_in.at[k, e, 2 + i3])
                 sources.append(r2(k, e, m2, i3))
             if m == 2:
                 arrived(r3(k, d, 0), rs3_in.at[k, d, 0])
@@ -315,26 +342,26 @@
     def send3(k, d, side, m):
         i3, h = source(r[k], side, m), half_of(side, m)
         ref = own[k].at[flat(p[k], q[k], h), i3]
-        send(k, 2, side, ref, ref, out3.at[k, d], in3.at[k, d, m])
+        send(k, 2, side, ref, ref, rs3_out.at[k, d], rs3_in.at[k, d, m])
 
     def send2(k, d, side, m, i3):
         i2, h = source(q[k], side, m), half_of(side, m)
         ref = own[k].at[flat(p[k], i2, h), i3]
-        send(k, 1, side, ref, ref, out2.at[k, d], in2.at[k, d, m, i3])
+        send(k, 1, side, ref, ref, rs2_out.at[k, d], rs2_in.at[k, d, (i3, 4, 5)[m]])
 
     def send1(k, d, side, m, i2):
         i1, h = source(p[k], side, m), half_of(side, m)
         ref = own[k].at[flat(i1, i2, h)]
-        send(k, 0, side, ref, ref, out1.at[k, d], in1.at[k, d, m, i2])
+        send(k, 0, side, ref, ref, rs1_out.at[k, d], rs1_in.at[k, d, (i2, 4, 5 + i2)[m]])
 
     def await3(k, d, m):
-        arrived(own[k].at[0, 0], in3.at[k, d, m])
-
-    def await2(k, d, m, i3):
-        arrived(own[k].at[0, 0], in2.at[k, d, m, i3])
+        arrived(own[k].at[0, 0], rs3_in.at[k, d, m])
+
+    def await2(k, d, i3):
+        arrived(own[k].at[0, 0], rs2_in.at[k, d, i3])
 
     def await1(k, d, m, i2):
-        arrived(own[k].at[0], in1.at[k, d, m, i2])
+        arrived(own[k].at[0], rs1_in.at[k, d, (i2, None, 5 + i2)[m]])
 
     def hand(k, i1, i2):
         both = pl.ds(flat(i1, i2, 0), 2)
@@ -398,38 +425,47 @@
 
     for offset in (0, -1, 1, 2):
         for k, d, side in lanes:
-            await2(k, d, 0, step(r[k], offset))
+            await2(k, d, step(r[k], offset))
             send2(k, d, side, 2, step(r[k], offset))
     for e, behind in enumerate(SIDES):
-        for offset in (0, -1, 1, 2):
-            for k in WEIGHTS:
-                await2(k, e, 1, step(r[k], offset))
+        for k in WEIGHTS:
+            arrived(own[k].at[0], rs2_in.at[k, e, 4])
         for m in range(2):
             for k, d, side in lanes:
                 send1(k, d, side, m, step(q[k], -behind))
         for k in WEIGHTS:
             hand(k, p[k], step(q[k], -behind))
-    for offset in (0, -1, 1, 2):
-        for k, d, side in lanes:
-            await2(k, d, 2, step(r[k], offset))
+    all_arrived(rs2_in, 5, False)
     for m in range(2):
         for k, d, side in lanes:
             send1(k, d, side, m, step(q[k], 2))
     for k in WEIGHTS:
         hand(k, p[k], step(q[k], 2))
-    for offset in (0, -1, 1, 2):
+    for offset in (0, -1, 1):
         for k, d, side in lanes:
             await1(k, d, 0, step(q[k], offset))
             send1(k, d, side, 2, step(q[k], offset))
+    for k, d, side in lanes:
+        await1(k, d, 0, step(q[k], 2))
+    for i3 in range(N):
+        for k, d, side in lanes:
+            ref = own[k].at[flat(source(p[k], side, 2), step(q[k], 2), half_of(side, 2)), i3]
+            send(k, 0, side, ref, ref, rs1_out.at[k, d], first_in.at[k, d, i3])
+    all_arrived(rs1_in, 4, True)
     for offset in (0, -1, 1, 2):
         for k, d, side in lanes:
-            await1(k, d, 1, step(q[k], offset))
             hand(k, step(p[k], -side), step(q[k], offset))
-    for offset in (0, -1, 1, 2):
+    for offset in (0, -1, 1):
         for k in WEIGHTS:
             for d in range(2):
                 await1(k, d, 2, step(q[k], offset))
             hand(k, step(p[k], 2), step(q[k], offset))
+    for i3 in range(N):
+        for k in WEIGHTS:
+            for d in range(2):
+                arrived(own[k].at[0, 0], first_in.at[k, d, i3])
+            both = pl.ds(flat(step(p[k], 2), step(q[k], 2), 0), 2)
+            push(own[k].at[both, i3], other[k].at[both, i3], pass_out.at[k], pass_in.at[k], partner)
 
     for k in WEIGHTS:
         arrived(own[k], part_out.at[k])
@@ -437,9 +473,9 @@
         for i in range(2):
             arrived(theirs[i][k], theirs_out.at[i, k])
         for d in range(2):
-            arrived(own[k].at[0:12], out1.at[k, d])
-            arrived(own[k].at[0:3], out2.at[k, d])
-            arrived(own[k].at[0, 0:3], out3.at[k, d])
+            arrived(own[k].at[0:12], rs1_out.at[k, d])
+            arrived(own[k].at[0:3], rs2_out.at[k, d])
+            arrived(own[k].at[0, 0:3], rs3_out.at[k, d])
         arrived(own[k], pass_out.at[k])
         arrived(other[k], pass_in.at[k])
 
@@ -493,16 +529,13 @@
             scratch_shapes=[
                 *each(2, 2, N), *each(2, 2), *(pltpu.VMEM(view[4:], bf16) for view in views),
                 *layer,
-                dma((3, 2 * N * N)), dma((3,)),
-                dma((3, 2, 3, N)), dma((3, 2)),
-                dma((3, 2, 3, N)), dma((3, 2)),
+                dma((3, 2, 6)), dma((3,)),
+                dma((3, 2, 9)), dma((3, 2)),
+                dma((3, 2, 6)), dma((3, 2)),
                 dma((3, 2, 3)), dma((3, 2)),
                 dma((3, 2, 2)),
                 dma((3,)), dma((2, 3)), dma((2, 3)), dma((2, 3)), dma((3,)), dma((3,)),
-                dma((3, 2, 3, N)), dma((3, 2)),
-                dma((3, 2, 3, N)), dma((3, 2)),
-                dma((3, 2, 3)), dma((3, 2)),
-                dma((3,)), dma((3,)), pltpu.SemaphoreType.REGULAR,
+                dma((3,)), dma((3,)), pltpu.SemaphoreType.REGULAR, dma((3, 2, N)),
             ],
             compiler_params=pltpu.CompilerParams(collective_id=0, has_side_effects=True, vmem_limit_bytes=LIMIT),
             name="step",

time: 221 us -> 220 us (level)
  no operation moved by 1% of the time
where the time goes in v4:
time: 220 us
  Pallas kernels  220 us (100%)
    pallas_call x1, Pallas kernels, step(): pl.pallas_call(step_kernel, out_shape=[*each(2 * N * N, N), *each(2 * N *...  203 us
    pallas_call x1, Pallas kernels, step(): pl.pallas_call(write_kernel, out_shape=[*(jax.ShapeDtypeStruct(view, bf16...  16.4 us

profile of v4, /device:TPU:1, one launch (start us, length us, event | category | flops | bytes accessed | tf_op | source)
XLA Modules:
  0.0 220.3 jit_solution(15132052246159676409)
XLA Ops:
  0.6 203.2 %step.1 = (bf16[32,4,8,4096]{3,2,1,0:T(8,128)(2,1)S(1)}, bf16[32,4,8,4096]{3,2,1,0:T(8,128)(2,1)S(1)}, bf16[32,4,64,512]{3,2,1,0:T(8,128)(2,1)S(1)}, bf16[32,4,8...) custom-call(bf16[2,4,4,4,8,8192]{5,4,3,2,1,0:T(8,128)(2,1)} %bitcast, ...), custom_call_target="tpu_custom_call" | custom-call | tf_op jit(solution)/shard_map/step/pallas_call | solution.py:524
  203.9 16.4 %write.1 = (bf16[2,4,4,4,8,8192]{5,4,3,2,1,0:T(8,128)(2,1)}, bf16[2,4,4,4,8,8192]{5,4,3,2,1,0:T(8,128)(2,1)}, bf16[2,4,4,4,2,64,512]{6,5,4,3,2,1,0:T(8,128)(2,1)...) custom-call(bf16[32,4,8,4096]{3,2,1,0:T(8,128)(2,1)S(1)} %get-tuple-, ...), custom_call_target="tpu_custom_call" | custom-call | tf_op jit(solution)/shard_map/write/pallas_call | solution.py:543

commit v5 on v3

--- a/solution.py
+++ b/solution.py
@@ -101,7 +101,7 @@
     theirs = (refs[33:36], refs[36:39])
     part_in, part_out, rs1_in, rs1_out, rs2_in, rs2_out, rs3_in, rs3_out, ahead_in = refs[39:48]
     weight_in, fresh_in, theirs_in, theirs_out, grad_in, grad_out = refs[48:54]
-    in1, out1, in2, out2, in3, out3, pass_in, pass_out, ready = refs[54:63]
+    pass_in, pass_out, ready, first_in, lead_in, lead_out = refs[54:60]
     chip, core = place()
     partner = device(chip, 1 - core)
     at = [[chip[axis] for axis in ORDER[k]] for k in WEIGHTS]
@@ -151,11 +151,24 @@
 
     small = [pltpu.make_async_copy(w[k].at[core, chip[0], chip[1], chip[2]], weight[k], weight_in.at[k]) for k in WEIGHTS]
     small += [pltpu.make_async_copy(moments[i][k], fresh[i][k], fresh_in.at[i, k]) for i in range(2) for k in WEIGHTS]
+    leads = []
+    for k, d, side in lanes:
+        i1, i2, h = spot(k, side, 0)
+        leads.append(pltpu.make_async_copy(piece(g[k], k, 1 - core, i1, i2, h), ahead[k].at[1, d], lead_in.at[k, d]))
+    for copy in leads:
+        copy.start()
     for copy in fetch(0):
         copy.start()
     greet(chip, core)
 
-    @pl.loop(0, N)
+    for i3 in range(N):
+        for (k, d, side), copy in zip(lanes, leads, strict=True):
+            i1, i2, h = spot(k, side, 0)
+            if i3 == 0:
+                copy.wait()
+            push(ahead[k].at[1, d, i3], own[k].at[flat(i1, i2, h), i3], lead_out.at[k], first_in.at[k, d, i3], partner)
+
+    @pl.loop(1, N)
     def _(t):
         give(t)
 
@@ -196,7 +209,26 @@
 
         return body
 
-    pl.loop(0, 2 * N)(first(False))
+    give(N)
+    pending = None
+    copies = fetch(0)
+    for i3 in range(N):
+        for k, d, side in lanes:
+            i1, i2, h = spot(k, side, 0)
+            if i3 == 0:
+                next(copies).wait()
+            here = own[k].at[flat(i1, i2, h), i3]
+            arrived(here, first_in.at[k, d, i3])
+            put_sum(here, [here, ahead[k].at[0, d, i3]])
+            if pending is not None:
+                pending()
+            pending = functools.partial(send, k, 0, side, here, r1(k, d, 0, i2).at[i3], rs1_out.at[k, d], rs1_in.at[k, d, 0, i2])
+    pending()
+    for k in WEIGHTS:
+        arrived(own[k].at[0:2], lead_out.at[k])
+    for copy in fetch(1):
+        copy.start()
+    pl.loop(1, 2 * N)(first(False))
     pl.loop(2 * N, 3 * N)(first(True))
 
     def fetch_kept(m):
@@ -315,26 +347,26 @@
     def send3(k, d, side, m):
         i3, h = source(r[k], side, m), half_of(side, m)
         ref = own[k].at[flat(p[k], q[k], h), i3]
-        send(k, 2, side, ref, ref, out3.at[k, d], in3.at[k, d, m])
+        send(k, 2, side, ref, ref, rs3_out.at[k, d], rs3_in.at[k, d, m])
 
     def send2(k, d, side, m, i3):
         i2, h = source(q[k], side, m), half_of(side, m)
         ref = own[k].at[flat(p[k], i2, h), i3]
-        send(k, 1, side, ref, ref, out2.at[k, d], in2.at[k, d, m, i3])
+        send(k, 1, side, ref, ref, rs2_out.at[k, d], rs2_in.at[k, d, m, i3])
 
     def send1(k, d, side, m, i2):
         i1, h = source(p[k], side, m), half_of(side, m)
         ref = own[k].at[flat(i1, i2, h)]
-        send(k, 0, side, ref, ref, out1.at[k, d], in1.at[k, d, m, i2])
+        send(k, 0, side, ref, ref, rs1_out.at[k, d], rs1_in.at[k, d, m, i2])
 
     def await3(k, d, m):
-        arrived(own[k].at[0, 0], in3.at[k, d, m])
+        arrived(own[k].at[0, 0], rs3_in.at[k, d, m])
 
     def await2(k, d, m, i3):
-        arrived(own[k].at[0, 0], in2.at[k, d, m, i3])
+        arrived(own[k].at[0, 0], rs2_in.at[k, d, m, i3])
 
     def await1(k, d, m, i2):
-        arrived(own[k].at[0], in1.at[k, d, m, i2])
+        arrived(own[k].at[0], rs1_in.at[k, d, m, i2])
 
     def hand(k, i1, i2):
         both = pl.ds(flat(i1, i2, 0), 2)
@@ -417,29 +449,41 @@
             send1(k, d, side, m, step(q[k], 2))
     for k in WEIGHTS:
         hand(k, p[k], step(q[k], 2))
-    for offset in (0, -1, 1, 2):
+    for offset in (0, -1, 1):
         for k, d, side in lanes:
             await1(k, d, 0, step(q[k], offset))
             send1(k, d, side, 2, step(q[k], offset))
+    for k, d, side in lanes:
+        await1(k, d, 0, step(q[k], 2))
+    for i3 in range(N):
+        for k, d, side in lanes:
+            ref = own[k].at[flat(source(p[k], side, 2), step(q[k], 2), half_of(side, 2)), i3]
+            send(k, 0, side, ref, ref, rs1_out.at[k, d], first_in.at[k, d, i3])
     for offset in (0, -1, 1, 2):
         for k, d, side in lanes:
             await1(k, d, 1, step(q[k], offset))
             hand(k, step(p[k], -side), step(q[k], offset))
-    for offset in (0, -1, 1, 2):
+    for offset in (0, -1, 1):
         for k in WEIGHTS:
             for d in range(2):
                 await1(k, d, 2, step(q[k], offset))
             hand(k, step(p[k], 2), step(q[k], offset))
-
-    for k in WEIGHTS:
-        arrived(own[k], part_out.at[k])
+    for i3 in range(N):
+        for k in WEIGHTS:
+            for d in range(2):
+                arrived(own[k].at[0, 0], first_in.at[k, d, i3])
+            both = pl.ds(flat(step(p[k], 2), step(q[k], 2), 0), 2)
+            push(own[k].at[both, i3], other[k].at[both, i3], pass_out.at[k], pass_in.at[k], partner)
+
+    for k in WEIGHTS:
+        arrived(own[k].at[0:30], part_out.at[k])
         arrived(grad[k].at[0], grad_out.at[k])
         for i in range(2):
             arrived(theirs[i][k], theirs_out.at[i, k])
         for d in range(2):
-            arrived(own[k].at[0:12], out1.at[k, d])
-            arrived(own[k].at[0:3], out2.at[k, d])
-            arrived(own[k].at[0, 0:3], out3.at[k, d])
+            arrived(own[k].at[0:12], rs1_out.at[k, d])
+            arrived(own[k].at[0:3], rs2_out.at[k, d])
+            arrived(own[k].at[0, 0:3], rs3_out.at[k, d])
         arrived(own[k], pass_out.at[k])
         arrived(other[k], pass_in.at[k])
 
@@ -499,10 +543,7 @@
                 dma((3, 2, 3)), dma((3, 2)),
                 dma((3, 2, 2)),
                 dma((3,)), dma((2, 3)), dma((2, 3)), dma((2, 3)), dma((3,)), dma((3,)),
-                dma((3, 2, 3, N)), dma((3, 2)),
-                dma((3, 2, 3, N)), dma((3, 2)),
-                dma((3, 2, 3)), dma((3, 2)),
-                dma((3,)), dma((3,)), pltpu.SemaphoreType.REGULAR,
+                dma((3,)), dma((3,)), pltpu.SemaphoreType.REGULAR, dma((3, 2, N)), dma((3, 2)), dma((3,)),
             ],
             compiler_params=pltpu.CompilerParams(collective_id=0, has_side_effects=True, vmem_limit_bytes=LIMIT),
             name="step",

time: 221 us -> 217 us (0.982)
  Pallas kernels: 220 us -> 216 us
    pallas_call x1, Pallas kernels: 204 us -> 199 us  [step(): pl.pallas_call(step_kernel, out_shape=[*each(2 * N * N, N), *each(2 * N *...]
where the time goes in v5:
time: 217 us; the launch traced here: 216 us
  Pallas kernels  216 us (100%)
    pallas_call x1, Pallas kernels, step(): pl.pallas_call(step_kernel, out_shape=[*each(2 * N * N, N), *each(2 * N *...  199 us
    pallas_call x1, Pallas kernels, step(): pl.pallas_call(write_kernel, out_shape=[*(jax.ShapeDtypeStruct(view, bf16...  16.4 us

profile of v5, /device:TPU:1, one launch (start us, length us, event | category | flops | bytes accessed | tf_op | source)
XLA Modules:
  0.0 216.4 jit_solution(8219280552379005768)
XLA Ops:
  0.6 199.3 %step.1 = (bf16[32,4,8,4096]{3,2,1,0:T(8,128)(2,1)S(1)}, bf16[32,4,8,4096]{3,2,1,0:T(8,128)(2,1)S(1)}, bf16[32,4,64,512]{3,2,1,0:T(8,128)(2,1)S(1)}, bf16[32,4,8...) custom-call(bf16[2,4,4,4,8,8192]{5,4,3,2,1,0:T(8,128)(2,1)} %bitcast, ...), custom_call_target="tpu_custom_call" | custom-call | tf_op jit(solution)/shard_map/step/pallas_call | solution.py:532
  200.0 16.4 %write.1 = (bf16[2,4,4,4,8,8192]{5,4,3,2,1,0:T(8,128)(2,1)}, bf16[2,4,4,4,8,8192]{5,4,3,2,1,0:T(8,128)(2,1)}, bf16[2,4,4,4,2,64,512]{6,5,4,3,2,1,0:T(8,128)(2,1)...) custom-call(bf16[32,4,8,4096]{3,2,1,0:T(8,128)(2,1)S(1)} %get-tuple-, ...), custom_call_target="tpu_custom_call" | custom-call | tf_op jit(solution)/shard_map/write/pallas_call | solution.py:551
